TPU v7x, 32 devices: a whole 2x2x4 slice. The times are simulated.
32 devices in a mesh: groups: 2 (over y), seq: 4 (over z), head: 4 (over x, core).
Axes of the slice: x: 2, y: 2, z: 4, core: 2. Of those that a mesh axis runs over, the one named last changes fastest.
Arguments:
- query: bfloat16 [4, 8192], P('groups', 'head'), parts along dimension 0, may hold values from -170 to 170
- cache_keys: bfloat16 [4, 1024, 1024], P('groups', 'seq', 'head'), parts along dimension 0, may hold values from -6 to 6
- cache_values: bfloat16 [4, 1024, 1024], P('groups', 'seq', 'head'), parts along dimension 0, may hold values from -6 to 6
- lengths: int32 [4], P('groups'), parts along dimension 0, may hold values from 256 to 1024
- heavy: int32 [4, 2], P('groups'), parts along dimension 0, may hold values from 0 to 7, as said below
- acc_scores: float32 [4, 8], P('groups', 'seq'), parts along dimension 0, may hold values from 0.01 to 1
- refill_kv: bfloat16 [64, 2, 128, 128], P(('groups', 'seq', 'head')), parts along dimension 0, may hold values from -6 to 6
- refill_dest: int32 [64, 1], P(('groups', 'seq', 'head')), parts along dimension 0, may hold values from 0 to 3, as said below
- refill_req: int32 [64], P(('groups', 'seq', 'head')), parts along dimension 0, may hold values from 0 to 1
- refill_head: int32 [64], P(('groups', 'seq', 'head')), parts along dimension 0, may hold values from 0 to 1
Outputs:
- attn_out: bfloat16 [4, 8192], P('groups'), parts along dimension 0
- block_scores: float32 [4, 8], P('groups', 'seq'), parts along dimension 0
- recalled_kv: bfloat16 [64, 2, 128, 128], P(('groups', 'seq', 'head')), parts along dimension 0
- recall_scores: float32 [32, 2], P(('groups', 'seq', 'head')), parts along dimension 0
There are 2 independent parts, one for each index of `groups`. A program takes and returns all parts, laid end to end along the dimension named above; each array names one. Nothing has to cross between parts.
Inputs may be any that keep to these rules, and one draw needn't show every extreme that they name: `heavy`: the 2 block ids of one request are distinct. `refill_dest`: the block at position j of device (s, h) goes to owner (s + k) mod 4, with k fixed by h and j alone; among the 2 blocks of one device at most 2 name the same owner, and on every device 2 do.
All inputs are finite; a program needn't handle non-finite values.
Results may differ from a plain program's by a relative error of at most 0.0045.
Values may be sent and summed in bfloat16 or wider, within the bound.
No kernel may reach another device: no remote copies, remote signals or barrier semaphores. Data moves between devices by JAX's collectives and lax.ppermute only.
A program may use at most 128 MiB of HBM per device.

v0:
```python
import math

import jax
import jax.numpy as jnp
from jax import lax
from jax.sharding import PartitionSpec as P

DH = 128
BLKTOK = 128
RECENT = 2
CAP = 2


NEG_BIG = -1e30


def joined(value, axis, join):
    pieces = jax.tree.map(lambda part: lax.all_gather(part, axis), value)
    head = jax.tree.map(lambda part: part[0], pieces)
    tail = jax.tree.map(lambda part: part[1:], pieces)
    subtotal, _ = lax.scan(lambda subtotal, share: (join(subtotal, share), None), head, tail)
    return subtotal


def combine_parts(first, second):
    best = jnp.maximum(first[0], second[0])
    weight_one = jnp.exp(first[0] - best)
    weight_two = jnp.exp(second[0] - best)
    return (
        best,
        first[1] * weight_one + second[1] * weight_two,
        first[2] * weight_one[..., None] + second[2] * weight_two[..., None],
    )


def on_device(
    query,
    cache_keys,
    cache_values,
    lengths,
    heavy,
    acc_scores,
    refill_kv,
    refill_dest,
    refill_req,
    refill_head,
):
    requests = query.shape[0]
    kv_local = cache_keys.shape[2] // DH
    heads_local = query.shape[1] // DH
    per_group = heads_local // kv_local
    seq_local = cache_keys.shape[1]
    blocks_local = seq_local // BLKTOK
    seq_count = lax.axis_size("seq")
    slots = seq_count * CAP
    score_scale = 1.0 / math.sqrt(DH)
    hiprec = lax.Precision.HIGHEST
    q_four = query.reshape(requests, kv_local, per_group, DH)
    keys_four = cache_keys.reshape(requests, seq_local, kv_local, DH)
    values_four = cache_values.reshape(requests, seq_local, kv_local, DH)
    seq_index = lax.axis_index("seq")
    owners = refill_dest[:, 0]
    held = refill_dest.shape[0]
    earlier = jnp.arange(held)[:, None] > jnp.arange(held)[None, :]
    order_in = jnp.sum((owners[:, None] == owners[None, :]) & earlier, axis=1)
    slot_of = owners * CAP + order_in
    steps_along = (owners - seq_index) % seq_count
    sender_of = (seq_index - steps_along) % seq_count
    pick = sender_of * CAP + order_in
    kv_buffer = (
        jnp.zeros((slots,) + refill_kv.shape[1:], refill_kv.dtype).at[slot_of].set(refill_kv)
    )
    got_kv = lax.all_to_all(
        kv_buffer.reshape((seq_count, CAP) + refill_kv.shape[1:]),
        "seq",
        split_axis=0,
        concat_axis=0,
        tiled=True,
    )
    recalled_kv = got_kv.reshape((slots,) + refill_kv.shape[1:])[pick]
    position = seq_index * seq_local + jnp.arange(seq_local, dtype=jnp.int32)
    block_ids = seq_index * blocks_local + jnp.arange(blocks_local, dtype=jnp.int32)
    heavy_hit = jnp.any(heavy[:, :, None] == block_ids[None, None, :], axis=1)
    recent = block_ids[None, :] >= ((lengths - 1) // BLKTOK - (RECENT - 1))[:, None]
    kept = jnp.repeat(heavy_hit | recent, BLKTOK, axis=1) & (position[None, :] < lengths[:, None])
    scores = (
        jnp.einsum("bkgd,btkd->bkgt", q_four, keys_four, preferred_element_type=jnp.float32)
        * score_scale
    )
    masked = jnp.where(kept[:, None, None, :], scores, NEG_BIG)
    valid = refill_req >= 0
    segment = jnp.maximum(refill_req, 0) * kv_local + refill_head
    member = (segment[:, None] == jnp.arange(requests * kv_local)[None, :]) & valid[:, None]
    member_f = member.astype(jnp.float32)
    q_units = q_four.reshape(requests * kv_local, per_group, DH)[segment]
    unit_scores = (
        jnp.einsum("ugd,urd->ugr", q_units, refill_kv[:, 0], preferred_element_type=jnp.float32)
        * score_scale
    )
    unit_scores = jnp.where(valid[:, None, None], unit_scores, NEG_BIG)
    unit_best = jnp.max(unit_scores, axis=2)
    seg_best = jnp.max(jnp.where(member[:, :, None], unit_best[:, None, :], NEG_BIG), axis=0)
    cache_best = jnp.max(masked, axis=3).reshape(requests * kv_local, per_group)
    local_max = jnp.maximum(cache_best, seg_best)
    cache_exp = jnp.where(
        kept[:, None, None, :],
        jnp.exp(masked - local_max.reshape(requests, kv_local, per_group, 1)),
        0.0,
    )
    unit_exp = jnp.where(
        valid[:, None, None], jnp.exp(unit_scores - local_max[segment][:, :, None]), 0.0
    )
    local_sum = jnp.sum(cache_exp, axis=3).reshape(requests * kv_local, per_group)
    local_sum = local_sum + jnp.dot(member_f.T, jnp.sum(unit_exp, axis=2), precision=hiprec)
    cache_acc = jnp.einsum(
        "bkgt,btkd->bkgd",
        cache_exp.astype(jnp.bfloat16),
        values_four,
        preferred_element_type=jnp.float32,
    )
    unit_pv = jnp.einsum(
        "ugr,urd->ugd",
        unit_exp.astype(jnp.bfloat16),
        refill_kv[:, 1],
        preferred_element_type=jnp.float32,
    )
    unit_acc = jnp.einsum("us,ugd->sgd", member_f, unit_pv, precision=hiprec)
    local_acc = cache_acc.reshape(requests * kv_local, per_group, DH) + unit_acc
    row_best, total, accum = joined((local_max, local_sum, local_acc), "seq", combine_parts)
    attn_local = (
        (accum / total[:, :, None]).astype(jnp.bfloat16).reshape(requests, heads_local * DH)
    )
    attn_out = lax.all_gather(attn_local, "head", axis=1, tiled=True)
    best_four = row_best.reshape(requests, kv_local, per_group, 1)
    total_four = total.reshape(requests, kv_local, per_group, 1)
    cache_prob = jnp.where(kept[:, None, None, :], jnp.exp(masked - best_four), 0.0) / total_four
    token_mass = jnp.sum(cache_prob, axis=(1, 2))
    block_local = token_mass.reshape(requests, blocks_local, BLKTOK).sum(axis=2)
    block_scores = acc_scores + lax.psum(block_local, "head")
    unit_prob = (
        jnp.where(valid[:, None, None], jnp.exp(unit_scores - row_best[segment][:, :, None]), 0.0)
        / total[segment][:, :, None]
    )
    unit_mass = jnp.sum(unit_prob, axis=(1, 2))
    mass_buffer = jnp.zeros((slots,), jnp.float32).at[slot_of].set(unit_mass)
    got_mass = lax.all_to_all(
        mass_buffer.reshape(seq_count, CAP), "seq", split_axis=0, concat_axis=0, tiled=True
    )
    recall_scores = got_mass.reshape(slots)[pick].reshape(1, held)
    return (attn_out, block_scores, recalled_kv, recall_scores)


def solution(mesh):
    in_specs = (
        P("groups", "head"),
        P("groups", "seq", "head"),
        P("groups", "seq", "head"),
        P("groups"),
        P("groups", None),
        P("groups", "seq"),
        P(("groups", "seq", "head"), None, None, None),
        P(("groups", "seq", "head"), None),
        P(("groups", "seq", "head")),
        P(("groups", "seq", "head")),
    )
    out_specs = (
        P("groups", None),
        P("groups", "seq"),
        P(("groups", "seq", "head"), None, None, None),
        P(("groups", "seq", "head"), None),
    )
    return jax.shard_map(
        on_device, mesh=mesh, in_specs=in_specs, out_specs=out_specs, check_vma=False
    )
```

profile of v0, /device:TPU:0, one launch (start us, length us, event | category | flops | bytes accessed | tf_op | source)
XLA Modules:
  0.0 80.1 jit_solution(16453932051277624068)
XLA Ops:
  0.7 0.7 copy-done.10
  1.4 0.6 copy-done.5
  2.0 0.7 copy-done.7
  3.0 0.4 copy-done.4
  3.6 0.6 gather_fusion
  4.1 1.1 %fusion.50 = (f32[2,8]{1,0:T(2,128)S(1)}, f32[2,8,128]{2,1,0:T(8,128)S(1)}) fusion(bf16[2,8,128]{2,1,0:T(8,128)(2,1)S(1)} %gather_fusion, bf16[2,2,128,128]{3,2,1,0:T(8,128)(2,1)} %param.18, pred[2]{0:T(512)(128)(4,1)S(1)} %broadcast_compare_fusion), kind=kOutput, calls=%fused_computation.99 | convolution fusion | flops 530416 | bytes 77890 | tf_op jit(solution)/shard_map/ugd,urd->ugr/dot_general | solution.py:97
  5.3 0.2 fusion.49
  5.6 0.6 gather_fusion.1
  6.6 13.6 %all-gather.2 = f32[4,4,8]{2,1,0:T(4,128)S(1)} all-gather(f32[1,4,8]{2,1,0:T(4,128)S(1)} %fusion.5), channel_id=2, replica_groups=mesh['groups'=2,'seq'=4,'head'=4] {'seq'}, dimensions={0}, use_global_device_ids=true | all-gather | bytes 640 | tf_op jit(solution)/shard_map/all_gather | solution.py:18
  20.3 0.6 copy-done.2
  20.9 11.9 %all_gather.19 = f32[4,4,8]{2,1,0:T(4,128)S(1)} all-gather(f32[1,4,8]{2,1,0:T(4,128)S(1)} %bitcast_maximum_fusion.1), channel_id=1, replica_groups=mesh['groups'=2,'seq'=4,'head'=4] {'seq'}, dimensions={0}, use_global_device_ids=true | all-gather | bytes 640 | tf_op jit(solution)/shard_map/all_gather | solution.py:18
  32.8 0.6 copy-done.3
  34.0 13.1 %all-gather.1 = f32[16,8,128]{2,1,0:T(8,128)S(1)} all-gather(f32[4,8,128]{2,1,0:T(8,128)S(1)} %bitcast_add_fusion), channel_id=3, replica_groups=mesh['groups'=2,'seq'=4,'head'=4] {'seq'}, dimensions={0}, use_global_device_ids=true | all-gather | bytes 81920 | tf_op jit(solution)/shard_map/all_gather | solution.py:18
  47.2 0.6 copy-done.8
  48.0 0.3 while.14
  48.4 0.6 gather_fusion.3
  48.9 0.6 gather_fusion.4
  49.7 0.6 scatter_custom_fusion.1
  50.2 0.7 all_to_all.10
  50.9 3.2 %all-to-all-start.1 = ((f32[4,1,2]{2,1,0:T(1,128)}), f32[4,1,2]{2,1,0:T(1,128)S(1)}, u32[]{:S(2)}, u32[]{:S(2)}) async-start(f32[4,1,2]{2,1,0:T(1,128)} %bitcast.24), calls=%async_computation.1 | async-start | bytes 4096 | tf_op jit(solution)/shard_map/all_to_all | solution.py:146
  54.1 0.9 %broadcast_in_dim.116 = bf16[8,2,128,128]{3,2,1,0:T(8,128)(2,1)} broadcast(bf16[]{:T(256)} %constant.74.clone.1), dimensions={} | broadcast | bytes 524290 | tf_op jit(solution)/shard_map/broadcast_in_dim | solution.py:71
  55.0 2.1 %scatter_fusion = bf16[8,2,128,128]{3,2,1,0:T(8,128)(2,1)} fusion(bf16[8,2,128,128]{3,2,1,0:T(8,128)(2,1)} %broadcast_in_dim.116, s32[2]{0:T(128)S(1)} %get-tuple-element.81, bf16[2,2,128,128]{3,2,1,0:T(8,128)(2,1)S(1)} %copy-done.1), kind=kCustom, calls=%fused_computation.6 | custom fusion | bytes 393224 | tf_op jit(solution)/shard_map/scatter | solution.py:71
  57.1 2.7 %all-to-all-done.1 = f32[4,1,2]{2,1,0:T(1,128)S(1)} async-done(((f32[4,1,2]{2,1,0:T(1,128)}), f32[4,1,2]{2,1,0:T(1,128)S(1)}, u32[]{:S(2)}, u32[]{:S(2)}) %all-to-all-start.1) | async-done | bytes 64 | tf_op jit(solution)/shard_map/all_to_all | solution.py:146
  59.8 4.4 %all-to-all-start = ((bf16[4,2,2,128,128]{4,3,2,1,0:T(8,128)(2,1)}), bf16[4,2,2,128,128]{4,3,2,1,0:T(8,128)(2,1)S(1)}, u32[]{:S(2)}, u32[]{:S(2)}) async-start(bf16[4,2,2,128,128]{4,3,2,1,0:T(8,128)(2,1)} %bitcast.21), calls=%async_computation | async-start | bytes 1048576 | tf_op jit(solution)/shard_map/all_to_all | solution.py:73
  64.4 5.6 %psum.7 = f32[2,2]{1,0:T(2,128)S(1)} all-reduce(f32[2,2]{1,0:T(2,128)S(1)} %reduce_sum.59), channel_id=1, replica_groups=mesh['groups'=2,'seq'=4,'head'=4] {'head'}, use_global_device_ids=true, to_apply=%region_10.11 | all-reduce | flops 4 | bytes 32 | tf_op jit(solution)/shard_map/psum | solution.py:139
  70.1 5.2 %all_gather.24 = bf16[2,8192]{1,0:T(2,128)(2,1)S(1)} all-gather(bf16[2,2048]{1,0:T(2,128)(2,1)S(1)} %reshape.178), channel_id=1, replica_groups=mesh['groups'=2,'seq'=4,'head'=4] {'head'}, dimensions={1}, use_global_device_ids=true | all-gather | bytes 40960 | tf_op jit(solution)/shard_map/all_gather | solution.py:133
  75.3 0.6 add.94
  75.9 0.5 broadcast.156
  76.4 0.7 reduce.3
  77.1 1.1 %gather_fusion.5 = f32[2]{0:T(128)} fusion(f32[8]{0:T(128)S(1)} %reshape.182, s32[1024]{0:T(1024)S(1)} %pad_clamp_fusion), kind=kCustom, calls=%fused_computation.5 | custom fusion | bytes 24 | tf_op jit(solution)/shard_map/gather | solution.py:149
  78.3 1.2 %gather_fusion.2 = bf16[2,2,128,128]{3,2,1,0:T(8,128)(2,1)} fusion(bf16[8,2,128,128]{3,2,1,0:T(8,128)(2,1)S(1)} %bitcast.99, s32[1024]{0:T(1024)S(1)} %pad_clamp_fusion), kind=kCustom, calls=%fused_computation.2 | custom fusion | bytes 262152 | tf_op jit(solution)/shard_map/gather | solution.py:80
  79.5 0.6 copy.91
  (64 shorter events, 2.8 us)
Async XLA Ops:
  0.6 4.6 %copy-start = (bf16[2,256,256]{2,1,0:T(8,128)(2,1)S(1)}, bf16[2,256,256]{2,1,0:T(8,128)(2,1)}, u32[]{:S(2)}) copy-start(bf16[2,256,256]{2,1,0:T(8,128)(2,1)} %param.13) | copy-start | bytes 786436
  0.7 0.7 copy-start.10
  1.4 0.7 copy-start.5
  2.0 0.7 copy-start.7
  2.0 0.9 %copy-start.9 = (s32[2]{0:T(128)S(1)}, s32[2]{0:T(128)}, u32[]{:S(2)}) copy-start(s32[2]{0:T(128)} %param.21) | copy-start | bytes 28
  2.7 0.7 copy-start.4
  5.3 28.5 %copy-start.11 = (bf16[2,256,256]{2,1,0:T(8,128)(2,1)S(1)}, bf16[2,256,256]{2,1,0:T(8,128)(2,1)}, u32[]{:S(2)}) copy-start(bf16[2,256,256]{2,1,0:T(8,128)(2,1)} %param.14) | copy-start | bytes 786436
  5.5 27.9 %copy-start.1 = (bf16[2,2,128,128]{3,2,1,0:T(8,128)(2,1)S(1)}, bf16[2,2,128,128]{3,2,1,0:T(8,128)(2,1)}, u32[]{:S(2)}) copy-start(bf16[2,2,128,128]{3,2,1,0:T(8,128)(2,1)} %param.18) | copy-start | bytes 393220
  20.3 0.6 copy-start.2
  32.8 0.6 copy-start.3
  47.2 0.7 copy-start.8
  47.2 0.9 %slice-start.1 = ((f32[4,4,8]{2,1,0:T(4,128)}), f32[3,4,8]{2,1,0:T(4,128)S(1)}, s32[]{:S(2)}) async-start(f32[4,4,8]{2,1,0:T(4,128)} %copy-done.3), calls=%async_computation.3 | async-start | bytes 12288 | tf_op jit(solution)/shard_map/slice | solution.py:20
  47.2 0.9 %slice-start = ((f32[4,4,8]{2,1,0:T(4,128)}), f32[3,4,8]{2,1,0:T(4,128)S(1)}, s32[]{:S(2)}) async-start(f32[4,4,8]{2,1,0:T(4,128)} %copy-done.2), calls=%async_computation.2 | async-start | bytes 12288 | tf_op jit(solution)/shard_map/slice | solution.py:20
  50.9 8.9 %all-to-all-start.1 = ((f32[4,1,2]{2,1,0:T(1,128)}), f32[4,1,2]{2,1,0:T(1,128)S(1)}, u32[]{:S(2)}, u32[]{:S(2)}) async-start(f32[4,1,2]{2,1,0:T(1,128)} %bitcast.24), calls=%async_computation.1 | async-start | bytes 4096 | tf_op jit(solution)/shard_map/all_to_all | solution.py:146
  59.8 18.5 %all-to-all-start = ((bf16[4,2,2,128,128]{4,3,2,1,0:T(8,128)(2,1)}), bf16[4,2,2,128,128]{4,3,2,1,0:T(8,128)(2,1)S(1)}, u32[]{:S(2)}, u32[]{:S(2)}) async-start(bf16[4,2,2,128,128]{4,3,2,1,0:T(8,128)(2,1)} %bitcast.21), calls=%async_computation | async-start | bytes 1048576 | tf_op jit(solution)/shard_map/all_to_all | solution.py:73
  70.1 5.2 %copy-start.6 = (f32[2,2]{1,0:T(2,128)S(1)}, f32[2,2]{1,0:T(2,128)}, u32[]{:S(2)}) copy-start(f32[2,2]{1,0:T(2,128)} %param.17) | copy-start | bytes 52
where the time goes:
time: 80.6 us; the launch traced here: 80.1 us
  blocking collectives  49.5 us (61%)
  local copies, waits for them, and re-layouts  14.4 us (18%)
  starting transfers between devices  7.6 us (9%)
  other arithmetic  2.95 us (4%)
  waiting for transfers between devices  2.7 us (3%)
  matrix products  2.09 us (3%)
  between operations  0.83 us (1%)
    all_gather x3, blocking collectives, joined(): pieces = jax.tree.map(lambda part: lax.all_gather(part, axis), value)  38.7 us
    psum x1, blocking collectives, on_device(): block_scores = acc_scores + lax.psum(block_local, 'head')  5.63 us
    all_gather x1, blocking collectives, on_device(): attn_out = lax.all_gather(attn_local, 'head', axis=1, tiled=True)  5.19 us
    unnamed x26, local copies, waits for them, and re-layouts  4.97 us
    all_to_all x1, starting transfers between devices, on_device(): lax.all_to_all(kv_buffer.reshape((seq_count, CAP) + refill_kv.shape[1:]),...  4.37 us
    all_to_all x1, starting transfers between devices, on_device(): lax.all_to_all(mass_buffer.reshape(seq_count, CAP), 'seq', split_axis=0,...  3.22 us
    all_to_all x1, waiting for transfers between devices, on_device(): lax.all_to_all(mass_buffer.reshape(seq_count, CAP), 'seq', split_axis=0,...  2.7 us
    scatter x1, local copies, waits for them, and re-layouts, on_device(): jnp.zeros((slots,) + refill_kv.shape[1:], refill_kv.dtype).at[slot_of]  2.06 us
  transfers between devices with their start and end apart: 2, of which 1 were waited for; matrix products, arithmetic and copies ran while one was open for 8% of the time, Pallas kernels for 0%

commit v1 on v0

v1 whole, which is shorter than its diff:
```python
import functools
import math

import jax
import jax.numpy as jnp
from jax import lax
from jax.experimental import pallas as pl
from jax.experimental.pallas import tpu as pltpu
from jax.sharding import PartitionSpec as P

DH = 128
BLKTOK = 128
RECENT = 2
CAP = 2
LANES = 128
FEW = 8

NEG_BIG = -1e30


def round_up(value, step):
    return (value + step - 1) // step * step


def by_flips(count):
    return 1 < count <= FEW and count & (count - 1) == 0


def flip(value, axis, mask):
    count = lax.axis_size(axis)
    return lax.ppermute(value, axis, [(at, at ^ mask) for at in range(count)])


def exchange(value, axis):
    count = lax.axis_size(axis)
    if by_flips(count):
        return (value,) + tuple(flip(value, axis, mask) for mask in range(1, count))
    return (lax.all_gather(value, axis),)


def pieces_of(refs, count):
    if len(refs) == count:
        return [ref[...] for ref in refs]
    return [refs[0][at] for at in range(count)]


def source_of(index, count, flips, at):
    return index ^ at if flips else jnp.int32(at)


def tree_sum(values):
    values = list(values)
    while len(values) > 1:
        pairs = [values[at] + values[at + 1] for at in range(0, len(values) - 1, 2)]
        if len(values) % 2:
            pairs.append(values[-1])
        values = pairs
    return values[0]


def nt_dot(left, right):
    return lax.dot_general(
        left, right, (((1,), (1,)), ((), ())), preferred_element_type=jnp.float32
    )


def nn_dot(left, right):
    return lax.dot_general(
        left, right, (((1,), (0,)), ((), ())), preferred_element_type=jnp.float32
    )


def local_kernel(
    lengths_hbm,
    heavy_hbm,
    req_hbm,
    head_hbm,
    query_hbm,
    keys_hbm,
    values_hbm,
    refill_hbm,
    part_ref,
    block_ref,
    lengths,
    heavy,
    req,
    unit_head,
    query,
    keys,
    values,
    refill,
    sems,
):
    pairs = (
        (lengths_hbm, lengths),
        (heavy_hbm, heavy),
        (req_hbm, req),
        (head_hbm, unit_head),
        (query_hbm, query),
        (keys_hbm, keys),
        (refill_hbm, refill),
        (values_hbm, values),
    )
    copies = [pltpu.make_async_copy(src, dst, sems.at[at]) for at, (src, dst) in enumerate(pairs)]
    for copy in copies:
        copy.start()
    requests, width = query.shape
    heads_local = width // DH
    seq_local = keys.shape[1]
    kv_local = keys.shape[2] // DH
    per_group = heads_local // kv_local
    held = refill.shape[0]
    nheavy = heavy.shape[1]
    blocks_local = seq_local // BLKTOK
    rows = heads_local * requests
    group_rows = per_group * requests
    score_scale = 1.0 / math.sqrt(DH)
    seq_index = lax.axis_index("seq")

    row = lax.broadcasted_iota(jnp.int32, (rows, 1), 0)
    row_req = lax.rem(row, requests)
    row_group = lax.div(row, group_rows)
    lane = lax.broadcasted_iota(jnp.int32, (1, seq_local), 1)
    position = lane + seq_index * seq_local
    lane_block = lax.div(lane, BLKTOK)
    for copy in copies[:4]:
        copy.wait()
    kept = None
    for b in range(requests):
        length = lengths[b]
        first_recent = lax.div(length - 1, BLKTOK) - (RECENT - 1)
        open_block = jnp.zeros((1, seq_local), jnp.int32)
        for j in range(blocks_local):
            block_id = seq_index * blocks_local + j
            hit = block_id >= first_recent
            for t in range(nheavy):
                hit = hit | (heavy[b, t] == block_id)
            open_block = jnp.where(lane_block == j, hit.astype(jnp.int32), open_block)
        kept_b = jnp.where(position < length, open_block, 0)
        kept_b = jnp.broadcast_to(kept_b, (rows, seq_local))
        kept = kept_b if kept is None else jnp.where(row_req == b, kept_b, kept)
    kept = kept > 0

    copies[4].wait()
    q_wide = query[...].astype(jnp.float32)
    q_rows = jnp.concatenate(
        [q_wide[:, i * DH : (i + 1) * DH] for i in range(heads_local)], axis=0
    ).astype(jnp.bfloat16)
    copies[5].wait()
    scores = []
    for g in range(kv_local):
        q_group = q_rows[g * group_rows : (g + 1) * group_rows]
        req_group = row_req[g * group_rows : (g + 1) * group_rows]
        found = None
        for b in range(requests):
            dots = nt_dot(q_group, keys[b, :, g * DH : (g + 1) * DH])
            found = dots if found is None else jnp.where(req_group == b, dots, found)
        scores.append(found)
    scores = jnp.concatenate(scores, axis=0) * score_scale
    masked = jnp.where(kept, scores, NEG_BIG)
    best = jnp.max(masked, axis=1, keepdims=True)

    copies[6].wait()
    unit_masked, unit_on = [], []
    for u in range(held):
        on = (row_group == unit_head[u]) & (row_req == req[u])
        dots = nt_dot(q_rows, refill[u, 0]) * score_scale
        dots = jnp.where(on, dots, NEG_BIG)
        unit_masked.append(dots)
        unit_on.append(on)
        best = jnp.maximum(best, jnp.max(dots, axis=1, keepdims=True))

    stat_lane = lax.broadcasted_iota(jnp.int32, (rows, LANES), 1)
    probs = jnp.where(kept, jnp.exp(masked - best), 0.0)
    total = jnp.sum(probs, axis=1, keepdims=True)
    block_cols = jnp.zeros((rows, LANES), jnp.float32)
    for j in range(blocks_local):
        mass = jnp.sum(probs[:, j * BLKTOK : (j + 1) * BLKTOK], axis=1, keepdims=True)
        block_cols = jnp.where(lax.rem(stat_lane, blocks_local) == j, mass, block_cols)
    block_ref[...] = block_cols
    stats = jnp.where(stat_lane == 0, best, 0.0)
    unit_probs = []
    for u in range(held):
        weight = jnp.where(unit_on[u], jnp.exp(unit_masked[u] - best), 0.0)
        mass = jnp.sum(weight, axis=1, keepdims=True)
        total = total + mass
        stats = jnp.where(stat_lane == 2 + u, mass, stats)
        unit_probs.append(weight.astype(jnp.bfloat16))
    stats = jnp.where(stat_lane == 1, total, stats)

    copies[7].wait()
    accum = []
    for g in range(kv_local):
        probs_group = probs[g * group_rows : (g + 1) * group_rows]
        req_group = row_req[g * group_rows : (g + 1) * group_rows]
        accum.append(
            tree_sum(
                nn_dot(
                    jnp.where(req_group == b, probs_group, 0.0).astype(jnp.bfloat16),
                    values[b, :, g * DH : (g + 1) * DH],
                )
                for b in range(requests)
            )
        )
    accum = jnp.concatenate(accum, axis=0)
    for u in range(held):
        accum = accum + nn_dot(unit_probs[u], refill[u, 1])
    part_ref[:rows, :] = accum
    stat_rows = part_ref.shape[0] - rows
    turned = jnp.transpose(stats)
    part_ref[rows:, :] = jnp.zeros((stat_rows, LANES), jnp.float32)
    part_ref[rows:, :rows] = turned[:stat_rows]


def middle_kernel(flips, count, rows, requests, blocks_local, dest, *refs):
    part_refs = refs[:-3]
    block_ref, head_ref, recall_ref = refs[-3:]
    held = dest.shape[0]
    seq_index = lax.axis_index("seq")
    pieces = pieces_of(part_refs, count)
    stat_rows = pieces[0].shape[0] - rows
    turned = jnp.transpose(jnp.concatenate([piece[rows:] for piece in pieces], axis=0))
    stats = [turned[:rows, at * stat_rows : (at + 1) * stat_rows] for at in range(count)]
    best = functools.reduce(jnp.maximum, [stat[:, 0:1] for stat in stats])
    factors = [jnp.exp(stat[:, 0:1] - best) for stat in stats]
    total = tree_sum(stat[:, 1:2] * factor for stat, factor in zip(stats, factors))
    accum = tree_sum(piece[:rows] * factor for piece, factor in zip(pieces, factors))
    head_ref[:rows, :] = (accum / total).astype(jnp.bfloat16)

    lane = lax.broadcasted_iota(jnp.int32, (1, held), 1)
    origin = jnp.zeros((1, held), jnp.int32)
    for j in range(held):
        steps = lax.rem(dest[j, 0] - seq_index + count, count)
        origin = jnp.where(lane == j, lax.rem(seq_index - steps + count, count), origin)
    recall = jnp.zeros((1, held), jnp.float32)
    for at in range(count):
        share = stats[at][:, 2 : 2 + held] * factors[at] / total
        mass = jnp.sum(share, axis=0, keepdims=True)
        recall = jnp.where(origin == source_of(seq_index, count, flips, at), mass, recall)
    recall_ref[...] = recall

    if flips:
        own = factors[0]
    else:
        own = functools.reduce(
            lambda found, at: jnp.where(seq_index == at, factors[at], found),
            range(1, count),
            factors[0],
        )
    row = lax.broadcasted_iota(jnp.int32, (rows, LANES), 0)
    lanes = lax.broadcasted_iota(jnp.int32, (rows, LANES), 1)
    mine = lax.rem(row, requests) == lax.div(lanes, blocks_local)
    mass = jnp.sum(jnp.where(mine, block_ref[...] * own / total, 0.0), axis=0, keepdims=True)
    high = mass.astype(jnp.bfloat16).astype(jnp.float32)
    middle = (mass - high).astype(jnp.bfloat16).astype(jnp.float32)
    low = mass - high - middle
    extra = head_ref.shape[0] - rows
    line = lax.broadcasted_iota(jnp.int32, (extra, LANES), 0)
    packed = jnp.where(line == 0, high, jnp.where(line == 1, middle, 0.0))
    packed = jnp.where(line == 2, low, packed)
    head_ref[rows:, :] = packed.astype(jnp.bfloat16)


def final_kernel(flips, count, rows, requests, acc_ref, *refs):
    piece_refs = refs[:-2]
    out_ref, block_ref = refs[-2:]
    head_index = lax.axis_index("head")
    blocks_local = acc_ref.shape[1]
    pieces = pieces_of(piece_refs, count)
    for at, piece in enumerate(pieces):
        start = source_of(head_index, count, flips, at) * rows
        out_ref[pl.ds(pl.multiple_of(start, rows), rows), :] = piece[:rows]
    masses = []
    for piece in pieces:
        lines = piece[rows:].astype(jnp.float32)
        masses.append(lines[0:1] + lines[1:2] + lines[2:3])
    mass = tree_sum(masses)
    lanes = lax.broadcasted_iota(jnp.int32, (1, LANES), 1)
    at_req = lax.broadcasted_iota(jnp.int32, (requests, blocks_local), 0)
    at_block = lax.broadcasted_iota(jnp.int32, (requests, blocks_local), 1)
    added = acc_ref[...]
    for b in range(requests):
        for j in range(blocks_local):
            one = jnp.sum(jnp.where(lanes == b * blocks_local + j, mass, 0.0), axis=1, keepdims=True)
            added = jnp.where((at_req == b) & (at_block == j), added + one, added)
    block_ref[...] = added


def move_blocks(refill_kv, owners, seq_index, seq_count):
    held = refill_kv.shape[0]
    steps = (owners - seq_index) % seq_count
    if held == CAP and seq_count == 1 << CAP:
        step = steps[0]
        high, low = seq_count // 2, 1
        across = flip(refill_kv, "seq", high)
        wanted = ((seq_index ^ low) - step) % seq_count
        passed = jnp.where(wanted == seq_index, refill_kv, across)
        beside = flip(passed, "seq", low)
        source = (seq_index - step) % seq_count
        return jnp.where(
            source == seq_index,
            refill_kv,
            jnp.where(source == seq_index ^ high, across, beside),
        )
    earlier = jnp.arange(held)[:, None] > jnp.arange(held)[None, :]
    order_in = jnp.sum((owners[:, None] == owners[None, :]) & earlier, axis=1)
    slots = seq_count * CAP
    slot_of = owners * CAP + order_in
    pick = (seq_index - steps) % seq_count * CAP + order_in
    buffer = jnp.zeros((slots,) + refill_kv.shape[1:], refill_kv.dtype).at[slot_of].set(refill_kv)
    got = lax.all_to_all(
        buffer.reshape((seq_count, CAP) + refill_kv.shape[1:]),
        "seq",
        split_axis=0,
        concat_axis=0,
        tiled=True,
    )
    return got.reshape((slots,) + refill_kv.shape[1:])[pick]


def on_device(
    query,
    cache_keys,
    cache_values,
    lengths,
    heavy,
    acc_scores,
    refill_kv,
    refill_dest,
    refill_req,
    refill_head,
):
    requests, width = query.shape
    heads_local = width // DH
    rows = heads_local * requests
    held = refill_kv.shape[0]
    blocks_local = cache_keys.shape[1] // BLKTOK
    seq_count = lax.axis_size("seq")
    head_count = lax.axis_size("head")
    seq_index = lax.axis_index("seq")
    hbm = pl.BlockSpec(memory_space=pl.ANY)
    vmem = pl.BlockSpec(memory_space=pltpu.VMEM)
    smem = pl.BlockSpec(memory_space=pltpu.SMEM)
    stat_rows = round_up(2 + held, 8)
    inputs = (lengths, heavy, refill_req, refill_head, query, cache_keys, cache_values, refill_kv)

    recalled_kv = move_blocks(refill_kv, refill_dest[:, 0], seq_index, seq_count)

    part, block_part = pl.pallas_call(
        local_kernel,
        out_shape=(
            jax.ShapeDtypeStruct((rows + stat_rows, LANES), jnp.float32),
            jax.ShapeDtypeStruct((rows, LANES), jnp.float32),
        ),
        in_specs=[hbm] * len(inputs),
        out_specs=(vmem, vmem),
        scratch_shapes=[pltpu.SMEM(value.shape, value.dtype) for value in inputs[:4]]
        + [pltpu.VMEM(value.shape, value.dtype) for value in inputs[4:]]
        + [pltpu.SemaphoreType.DMA((len(inputs),))],
        name="local_attention",
    )(*inputs)

    parts = exchange(part, "seq")
    head_part, recall_scores = pl.pallas_call(
        functools.partial(
            middle_kernel, by_flips(seq_count), seq_count, rows, requests, blocks_local
        ),
        out_shape=(
            jax.ShapeDtypeStruct((rows + 16, LANES), jnp.bfloat16),
            jax.ShapeDtypeStruct((1, held), jnp.float32),
        ),
        in_specs=[smem] + [vmem] * (len(parts) + 1),
        out_specs=(vmem, vmem),
        name="combine_seq",
    )(refill_dest, *parts, block_part)

    head_parts = exchange(head_part, "head")
    attn_rows, block_scores = pl.pallas_call(
        functools.partial(final_kernel, by_flips(head_count), head_count, rows, requests),
        out_shape=(
            jax.ShapeDtypeStruct((head_count * rows, LANES), jnp.bfloat16),
            jax.ShapeDtypeStruct(acc_scores.shape, jnp.float32),
        ),
        in_specs=[vmem] * (len(head_parts) + 1),
        out_specs=(vmem, vmem),
        name="join_heads",
    )(acc_scores, *head_parts)
    attn_out = (
        attn_rows.reshape(head_count * heads_local, requests, DH)
        .transpose(1, 0, 2)
        .reshape(requests, head_count * width)
    )
    return (attn_out, block_scores, recalled_kv, recall_scores)


def solution(mesh):
    in_specs = (
        P("groups", "head"),
        P("groups", "seq", "head"),
        P("groups", "seq", "head"),
        P("groups"),
        P("groups", None),
        P("groups", "seq"),
        P(("groups", "seq", "head"), None, None, None),
        P(("groups", "seq", "head"), None),
        P(("groups", "seq", "head")),
        P(("groups", "seq", "head")),
    )
    out_specs = (
        P("groups", None),
        P("groups", "seq"),
        P(("groups", "seq", "head"), None, None, None),
        P(("groups", "seq", "head"), None),
    )
    return jax.shard_map(
        on_device, mesh=mesh, in_specs=in_specs, out_specs=out_specs, check_vma=False
    )
```

time: 80.6 us -> 34.6 us (0.43)
  blocking collectives: 49.5 us -> 0 us
  local copies, waits for them, and re-layouts: 14.4 us -> 2.53 us
  waiting for transfers between devices: 2.7 us -> 12.4 us
  Pallas kernels: 0 us -> 5.81 us
  starting transfers between devices: 7.6 us -> 10.8 us
  matrix products: 2.09 us -> 0 us
  other arithmetic: 2.95 us -> 1.61 us
    all_gather x4 -> x0, blocking collectives: 43.9 us -> none  [the longest x3 38.7 us: joined(): pieces = jax.tree.map(lambda part: lax.all_gather(part, axis), value)]
    ppermute x0 -> x8, waiting for transfers between devices: none -> 12.4 us  [flip(): return lax.ppermute(value, axis, [(at, at ^ mask) for at in range(count)])]
    ppermute x0 -> x8, starting transfers between devices: none -> 10.8 us  [flip(): return lax.ppermute(value, axis, [(at, at ^ mask) for at in range(count)])]
    all_to_all x2 -> x0, starting transfers between devices: 7.6 us -> none  [the longest x1 4.37 us: on_device(): lax.all_to_all(kv_buffer.reshape((seq_count, CAP) + refill_kv.shape[1:]),...]
    pallas_call x0 -> x3, Pallas kernels: none -> 5.81 us  [the longest x1 2.42 us: on_device(): pl.pallas_call(local_kernel, out_shape=(jax.ShapeDtypeStruct((rows + stat...]
    psum x1 -> x0, blocking collectives: 5.63 us -> none  [on_device(): block_scores = acc_scores + lax.psum(block_local, 'head')]
    gather x6 -> x0, local copies, waits for them, and re-layouts: 4.6 us -> none  [the longest x1 1.22 us: on_device(): recalled_kv = got_kv.reshape((slots,) + refill_kv.shape[1:])[pick]]
    all_to_all x2 -> x0, waiting for transfers between devices: 2.7 us -> none  [the longest x1 2.7 us: on_device(): lax.all_to_all(mass_buffer.reshape(seq_count, CAP), 'seq', split_axis=0,...]
  transfers between devices with their start and end apart: 2 -> 8, of which waited for: 1 -> 5; matrix products, arithmetic and copies ran while one was open for 8% -> 2% of each run, Pallas kernels for 0% -> 17%
where the time goes in v1:
time: 34.6 us; the launch traced here: 33.9 us
  waiting for transfers between devices  12.4 us (36%)
  starting transfers between devices  10.8 us (31%)
  Pallas kernels  5.81 us (17%)
  local copies, waits for them, and re-layouts  2.53 us (7%)
  other arithmetic  1.61 us (5%)
  between operations  0.81 us (2%)
    ppermute x8, waiting for transfers between devices, flip(): return lax.ppermute(value, axis, [(at, at ^ mask) for at in range(count)])  12.4 us
    ppermute x8, starting transfers between devices, flip(): return lax.ppermute(value, axis, [(at, at ^ mask) for at in range(count)])  10.8 us
    unnamed x17, local copies, waits for them, and re-layouts  2.53 us
    pallas_call x1, Pallas kernels, on_device(): pl.pallas_call(local_kernel, out_shape=(jax.ShapeDtypeStruct((rows + stat...  2.42 us
    pallas_call x1, Pallas kernels, on_device(): pl.pallas_call(functools.partial(middle_kernel, by_flips(seq_count), seq_...  1.95 us
    pallas_call x1, Pallas kernels, on_device(): pl.pallas_call(functools.partial(final_kernel, by_flips(head_count), head...  1.43 us
    select_n x1, other arithmetic, move_blocks(): passed = jnp.where(wanted == seq_index, refill_kv, across)  0.92 us
  transfers between devices with their start and end apart: 8, of which 5 were waited for; matrix products, arithmetic and copies ran while one was open for 2% of the time, Pallas kernels for 17%

profile of v1, /device:TPU:0, one launch (start us, length us, event | category | flops | bytes accessed | tf_op | source)
XLA Modules:
  0.0 33.9 jit_solution(5318850249707476986)
XLA Ops:
  0.6 4.1 %collective-permute-start.6 = (bf16[2,2,128,128]{3,2,1,0:T(8,128)(2,1)}, bf16[2,2,128,128]{3,2,1,0:T(8,128)(2,1)S(1)}, u32[]{:S(2)}, u32[]{:S(2)}) collective-permute-start(bf16[2,2,128,128]{3,2,1,0:T(8,128)(2,1)} %refill_hbm.1), channel_id=1, source_target_pairs={{0,8},{4,12},{8,0},{12,4},{1,9},{5,13},{9,1},{13,5},{2,10},{6,14},... | collective-permute-start | bytes 393224 | tf_op jit(solution)/shard_map/ppermute | solution.py:31
  4.8 0.7 %copy-done.7 = s32[2,1]{0,1:T(1,128)S(1)} copy-done((s32[2,1]{0,1:T(1,128)S(1)}, s32[2,1]{0,1:T(1,128)}, u32[]{:S(2)}) %copy-start.7) | copy-done | bytes 32
  5.5 5.8 %collective-permute-done.6 = bf16[2,2,128,128]{3,2,1,0:T(8,128)(2,1)S(1)} collective-permute-done((bf16[2,2,128,128]{3,2,1,0:T(8,128)(2,1)}, bf16[2,2,128,128]{3,2,1,0:T(8,128)(2,1)S(1)}, u32[]{:S(2)}, u32[]{:S(2)}) %collective-permute-start.6) | collective-permute-done | bytes 131104 | tf_op jit(solution)/shard_map/ppermute | solution.py:31
  11.3 0.9 %broadcast_select_fusion = bf16[2,2,128,128]{3,2,1,0:T(8,128)(2,1)S(1)} fusion(bf16[2,2,128,128]{3,2,1,0:T(8,128)(2,1)} %refill_hbm.1, bf16[2,2,128,128]{3,2,1,0:T(8,128)(2,1)S(1)} %collective-permute-done.6, pred[]{:T(512)S(6)} %eq.16), kind=kLoop, calls=%fused_computation.1 | loop fusion | flops 65536 | bytes 393217 | tf_op jit(solution)/shard_map/jit(_where)/select_n | solution.py:297
  12.2 0.1 collective-permute-start.7
  12.3 2.4 %local_attention.1 = (f32[40,128]{1,0:T(8,128)}, f32[32,128]{1,0:T(8,128)}) custom-call(s32[2]{0:T(128)} %lengths_hbm.1, s32[2,2]{1,0:T(2,128)} %heavy_hbm.1, s32[2]{0:T(128)} %req_hbm.1, s32[2]{0:T(128)} %head_hbm.1, bf16[2,2048]{1,0:T(2,128)(2,1)} %query_hbm.1, bf16[2,256,256]{2,1,0:T(8,128)(2,1)} %keys_hbm.1, bf16[2,256,256]{2,1,0:T(8,128)(2,1)} %values_hbm.1, ...), custom_call_target="tpu_custom_call" | custom-call | tf_op jit(solution)/shard_map/local_attention/pallas_call | solution.py:349
  14.7 0.0 copy-start
  14.7 2.1 %collective-permute-start = (f32[40,128]{1,0:T(8,128)}, f32[40,128]{1,0:T(8,128)S(1)}, u32[]{:S(2)}, u32[]{:S(2)}) collective-permute-start(f32[40,128]{1,0:T(8,128)} %get-tuple-element.10.refs_0_), channel_id=1, source_target_pairs={{0,4},{4,0},{8,12},{12,8},{1,5},{5,1},{9,13},{13,9},{2,6},{6,2},{1... | collective-permute-start | bytes 61448 | tf_op jit(solution)/shard_map/ppermute | solution.py:31
  16.8 1.3 %collective-permute-start.1 = (f32[40,128]{1,0:T(8,128)}, f32[40,128]{1,0:T(8,128)S(1)}, u32[]{:S(2)}, u32[]{:S(2)}) collective-permute-start(f32[40,128]{1,0:T(8,128)} %get-tuple-element.10.refs_0_), channel_id=1, source_target_pairs={{0,8},{4,12},{8,0},{12,4},{1,9},{5,13},{9,1},{13,5},{2,10},{6,14},... | collective-permute-start | bytes 61448 | tf_op jit(solution)/shard_map/ppermute | solution.py:31
  18.0 1.4 %collective-permute-start.2 = (f32[40,128]{1,0:T(8,128)}, f32[40,128]{1,0:T(8,128)S(1)}, u32[]{:S(2)}, u32[]{:S(2)}) collective-permute-start(f32[40,128]{1,0:T(8,128)} %get-tuple-element.10.refs_0_), channel_id=1, source_target_pairs={{0,12},{4,8},{8,4},{12,0},{1,13},{5,9},{9,5},{13,1},{2,14},{6,10},... | collective-permute-start | bytes 61448 | tf_op jit(solution)/shard_map/ppermute | solution.py:31
  19.4 0.6 %copy.14.dest = s32[2,1]{1,0:T(2,128)} copy(s32[2,1]{0,1:T(1,128)S(1)} %copy-done.7) | data formatting | bytes 16 | tf_op args[7]
  20.1 0.0 collective-permute-done.refs_1_
  20.1 1.8 %collective-permute-done.1.refs_2_ = f32[40,128]{1,0:T(8,128)S(1)} collective-permute-done((f32[40,128]{1,0:T(8,128)}, f32[40,128]{1,0:T(8,128)S(1)}, u32[]{:S(2)}, u32[]{:S(2)}) %collective-permute-start.1) | collective-permute-done | bytes 20512 | tf_op jit(solution)/shard_map/ppermute | solution.py:31
  21.9 1.9 %collective-permute-done.2.refs_3_ = f32[40,128]{1,0:T(8,128)S(1)} collective-permute-done((f32[40,128]{1,0:T(8,128)}, f32[40,128]{1,0:T(8,128)S(1)}, u32[]{:S(2)}, u32[]{:S(2)}) %collective-permute-start.2) | collective-permute-done | bytes 20512 | tf_op jit(solution)/shard_map/ppermute | solution.py:31
  23.8 0.0 copy-done.1
  23.8 0.0 copy-done.2
  23.8 0.6 %copy-done.3 = f32[40,128]{1,0:T(8,128)} copy-done((f32[40,128]{1,0:T(8,128)}, f32[40,128]{1,0:T(8,128)S(1)}, u32[]{:S(2)}) %copy-start.3) | copy-done | bytes 20504
  24.4 2.0 %combine_seq.1 = (bf16[48,128]{1,0:T(8,128)(2,1)}, f32[1,2]{1,0:T(1,128)}) custom-call(s32[2,1]{1,0:T(2,128)} %copy.14.dest, f32[40,128]{1,0:T(8,128)} %get-tuple-element.10.refs_0_, f32[40,128]{1,0:T(8,128)} %copy-done.1, f32[40,128]{1,0:T(8,128)} %copy-done.2, f32[40,128]{1,0:T(8,128)} %copy-done.3, f32[32,128]{1,0:T(8,128)} %get-tuple-element.11.refs_4_), custom_call_target="tpu_custom_call" | custom-call | tf_op jit(solution)/shard_map/combine_seq/pallas_call | solution.py:364
  26.4 0.0 collective-permute-start.3
  26.4 1.5 %collective-permute-start.4 = (bf16[48,128]{1,0:T(8,128)(2,1)}, bf16[48,128]{1,0:T(8,128)(2,1)S(1)}, u32[]{:S(2)}, u32[]{:S(2)}) collective-permute-start(bf16[48,128]{1,0:T(8,128)(2,1)} %get-tuple-element.12.refs_0_), channel_id=1, source_target_pairs={{0,2},{1,3},{2,0},{3,1},{4,6},{5,7},{6,4},{7,5},{8,10},{9,11},{10,... | collective-permute-start | bytes 36872 | tf_op jit(solution)/shard_map/ppermute | solution.py:31
  27.9 0.4 %collective-permute-start.5 = (bf16[48,128]{1,0:T(8,128)(2,1)}, bf16[48,128]{1,0:T(8,128)(2,1)S(1)}, u32[]{:S(2)}, u32[]{:S(2)}) collective-permute-start(bf16[48,128]{1,0:T(8,128)(2,1)} %get-tuple-element.12.refs_0_), channel_id=1, source_target_pairs={{0,3},{1,2},{2,1},{3,0},{4,7},{5,6},{6,5},{7,4},{8,11},{9,10},{10,... | collective-permute-start | bytes 36872 | tf_op jit(solution)/shard_map/ppermute | solution.py:31
  28.3 0.0 collective-permute-done.3.refs_1_
  28.3 0.0 copy-start.4
  28.3 2.0 %collective-permute-done.4.refs_2_ = bf16[48,128]{1,0:T(8,128)(2,1)S(1)} collective-permute-done((bf16[48,128]{1,0:T(8,128)(2,1)}, bf16[48,128]{1,0:T(8,128)(2,1)S(1)}, u32[]{:S(2)}, u32[]{:S(2)}) %collective-permute-start.4) | collective-permute-done | bytes 12320 | tf_op jit(solution)/shard_map/ppermute | solution.py:31
  30.3 0.9 %collective-permute-done.5.refs_3_ = bf16[48,128]{1,0:T(8,128)(2,1)S(1)} collective-permute-done((bf16[48,128]{1,0:T(8,128)(2,1)}, bf16[48,128]{1,0:T(8,128)(2,1)S(1)}, u32[]{:S(2)}, u32[]{:S(2)}) %collective-permute-start.5) | collective-permute-done | bytes 12320 | tf_op jit(solution)/shard_map/ppermute | solution.py:31
  31.2 0.0 copy-done.4
  31.2 0.0 copy-done.5
  31.2 0.6 %copy-done.6 = bf16[48,128]{1,0:T(8,128)(2,1)} copy-done((bf16[48,128]{1,0:T(8,128)(2,1)}, bf16[48,128]{1,0:T(8,128)(2,1)S(1)}, u32[]{:S(2)}) %copy-start.6) | copy-done | bytes 12312
  31.8 1.4 %join_heads.1 = (bf16[128,128]{1,0:T(8,128)(2,1)}, f32[2,2]{1,0:T(2,128)}) custom-call(f32[2,2]{1,0:T(2,128)} %acc_ref.1, bf16[48,128]{1,0:T(8,128)(2,1)} %get-tuple-element.12.refs_0_, bf16[48,128]{1,0:T(8,128)(2,1)} %copy-done.4, bf16[48,128]{1,0:T(8,128)(2,1)} %copy-done.5, bf16[48,128]{1,0:T(8,128)(2,1)} %copy-done.6), custom_call_target="tpu_custom_call" | custom-call | tf_op jit(solution)/shard_map/join_heads/pallas_call | solution.py:378
  33.3 0.0 collective-permute-done.7
  33.3 0.0 copy-done
  33.3 0.7 %select_select_fusion = bf16[2,2,128,128]{3,2,1,0:T(8,128)(2,1)} fusion(bf16[2,2,128,128]{3,2,1,0:T(8,128)(2,1)S(1)} %copy-done, bf16[2,2,128,128]{3,2,1,0:T(8,128)(2,1)S(1)} %collective-permute-done.6, bf16[2,2,128,128]{3,2,1,0:T(8,128)(2,1)S(1)} %collective-permute-done.7, pred[]{:T(512)S(6)} %eq.15, pred[]{:T(512)S(6)} %eq.14), kind=kLoop, calls=%fused_computation | loop fusion | flops 131072 | bytes 524290 | tf_op jit(solution)/shard_map/jit(_where)/select_n | solution.py:300
  (7 shorter events, 0.0 us)
Async XLA Ops:
  0.6 10.6 %collective-permute-start.6 = (bf16[2,2,128,128]{3,2,1,0:T(8,128)(2,1)}, bf16[2,2,128,128]{3,2,1,0:T(8,128)(2,1)S(1)}, u32[]{:S(2)}, u32[]{:S(2)}) collective-permute-start(bf16[2,2,128,128]{3,2,1,0:T(8,128)(2,1)} %refill_hbm.1), channel_id=1, source_target_pairs={{0,8},{4,12},{8,0},{12,4},{1,9},{5,13},{9,1},{13,5},{2,10},{6,14},... | collective-permute-start | bytes 393224 | tf_op jit(solution)/shard_map/ppermute | solution.py:31
  4.8 0.7 %copy-start.7 = (s32[2,1]{0,1:T(1,128)S(1)}, s32[2,1]{0,1:T(1,128)}, u32[]{:S(2)}) copy-start(s32[2,1]{0,1:T(1,128)} %param.17) | copy-start | bytes 28
  12.2 21.1 %collective-permute-start.7 = (bf16[2,2,128,128]{3,2,1,0:T(8,128)(2,1)S(1)}, bf16[2,2,128,128]{3,2,1,0:T(8,128)(2,1)S(1)}, u32[]{:S(2)}, u32[]{:S(2)}) collective-permute-start(bf16[2,2,128,128]{3,2,1,0:T(8,128)(2,1)S(1)} %broadcast_select_fusion), channel_id=1, source_target_pairs={{0,4},{4,0},{8,12},{12,8},{1,5},{5,1},{9,13},{13,9},{2,6},{6,2},{1... | collective-permute-start | bytes 393224 | tf_op jit(solution)/shard_map/ppermute | solution.py:31
  14.7 18.6 %copy-start = (bf16[2,2,128,128]{3,2,1,0:T(8,128)(2,1)S(1)}, bf16[2,2,128,128]{3,2,1,0:T(8,128)(2,1)}, u32[]{:S(2)}) copy-start(bf16[2,2,128,128]{3,2,1,0:T(8,128)(2,1)} %refill_hbm.1) | copy-start | bytes 393220
  14.7 5.4 %collective-permute-start = (f32[40,128]{1,0:T(8,128)}, f32[40,128]{1,0:T(8,128)S(1)}, u32[]{:S(2)}, u32[]{:S(2)}) collective-permute-start(f32[40,128]{1,0:T(8,128)} %get-tuple-element.10.refs_0_), channel_id=1, source_target_pairs={{0,4},{4,0},{8,12},{12,8},{1,5},{5,1},{9,13},{13,9},{2,6},{6,2},{1... | collective-permute-start | bytes 61448 | tf_op jit(solution)/shard_map/ppermute | solution.py:31
  16.8 5.1 %collective-permute-start.1 = (f32[40,128]{1,0:T(8,128)}, f32[40,128]{1,0:T(8,128)S(1)}, u32[]{:S(2)}, u32[]{:S(2)}) collective-permute-start(f32[40,128]{1,0:T(8,128)} %get-tuple-element.10.refs_0_), channel_id=1, source_target_pairs={{0,8},{4,12},{8,0},{12,4},{1,9},{5,13},{9,1},{13,5},{2,10},{6,14},... | collective-permute-start | bytes 61448 | tf_op jit(solution)/shard_map/ppermute | solution.py:31
  18.0 5.8 %collective-permute-start.2 = (f32[40,128]{1,0:T(8,128)}, f32[40,128]{1,0:T(8,128)S(1)}, u32[]{:S(2)}, u32[]{:S(2)}) collective-permute-start(f32[40,128]{1,0:T(8,128)} %get-tuple-element.10.refs_0_), channel_id=1, source_target_pairs={{0,12},{4,8},{8,4},{12,0},{1,13},{5,9},{9,5},{13,1},{2,14},{6,10},... | collective-permute-start | bytes 61448 | tf_op jit(solution)/shard_map/ppermute | solution.py:31
  20.1 3.8 %copy-start.1 = (f32[40,128]{1,0:T(8,128)}, f32[40,128]{1,0:T(8,128)S(1)}, u32[]{:S(2)}) copy-start(f32[40,128]{1,0:T(8,128)S(1)} %collective-permute-done.refs_1_) | copy-start | bytes 61444
  21.9 1.9 %copy-start.2 = (f32[40,128]{1,0:T(8,128)}, f32[40,128]{1,0:T(8,128)S(1)}, u32[]{:S(2)}) copy-start(f32[40,128]{1,0:T(8,128)S(1)} %collective-permute-done.1.refs_2_) | copy-start | bytes 61444
  23.8 0.6 %copy-start.3 = (f32[40,128]{1,0:T(8,128)}, f32[40,128]{1,0:T(8,128)S(1)}, u32[]{:S(2)}) copy-start(f32[40,128]{1,0:T(8,128)S(1)} %collective-permute-done.2.refs_3_) | copy-start | bytes 61444
  26.4 1.9 %collective-permute-start.3 = (bf16[48,128]{1,0:T(8,128)(2,1)}, bf16[48,128]{1,0:T(8,128)(2,1)S(1)}, u32[]{:S(2)}, u32[]{:S(2)}) collective-permute-start(bf16[48,128]{1,0:T(8,128)(2,1)} %get-tuple-element.12.refs_0_), channel_id=1, source_target_pairs={{0,1},{1,0},{2,3},{3,2},{4,5},{5,4},{6,7},{7,6},{8,9},{9,8},{10,11... | collective-permute-start | bytes 36872 | tf_op jit(solution)/shard_map/ppermute | solution.py:31
  26.4 3.9 %collective-permute-start.4 = (bf16[48,128]{1,0:T(8,128)(2,1)}, bf16[48,128]{1,0:T(8,128)(2,1)S(1)}, u32[]{:S(2)}, u32[]{:S(2)}) collective-permute-start(bf16[48,128]{1,0:T(8,128)(2,1)} %get-tuple-element.12.refs_0_), channel_id=1, source_target_pairs={{0,2},{1,3},{2,0},{3,1},{4,6},{5,7},{6,4},{7,5},{8,10},{9,11},{10,... | collective-permute-start | bytes 36872 | tf_op jit(solution)/shard_map/ppermute | solution.py:31
  27.9 3.3 %collective-permute-start.5 = (bf16[48,128]{1,0:T(8,128)(2,1)}, bf16[48,128]{1,0:T(8,128)(2,1)S(1)}, u32[]{:S(2)}, u32[]{:S(2)}) collective-permute-start(bf16[48,128]{1,0:T(8,128)(2,1)} %get-tuple-element.12.refs_0_), channel_id=1, source_target_pairs={{0,3},{1,2},{2,1},{3,0},{4,7},{5,6},{6,5},{7,4},{8,11},{9,10},{10,... | collective-permute-start | bytes 36872 | tf_op jit(solution)/shard_map/ppermute | solution.py:31
  28.3 2.9 %copy-start.4 = (bf16[48,128]{1,0:T(8,128)(2,1)}, bf16[48,128]{1,0:T(8,128)(2,1)S(1)}, u32[]{:S(2)}) copy-start(bf16[48,128]{1,0:T(8,128)(2,1)S(1)} %collective-permute-done.3.refs_1_) | copy-start | bytes 36868
  30.3 0.9 %copy-start.5 = (bf16[48,128]{1,0:T(8,128)(2,1)}, bf16[48,128]{1,0:T(8,128)(2,1)S(1)}, u32[]{:S(2)}) copy-start(bf16[48,128]{1,0:T(8,128)(2,1)S(1)} %collective-permute-done.4.refs_2_) | copy-start | bytes 36868
  31.2 0.6 %copy-start.6 = (bf16[48,128]{1,0:T(8,128)(2,1)}, bf16[48,128]{1,0:T(8,128)(2,1)S(1)}, u32[]{:S(2)}) copy-start(bf16[48,128]{1,0:T(8,128)(2,1)S(1)} %collective-permute-done.5.refs_3_) | copy-start | bytes 36868

commit v2 on v1

--- a/solution.py
+++ b/solution.py
@@ -8,6 +8,7 @@
 from jax.experimental.pallas import tpu as pltpu
 from jax.sharding import PartitionSpec as P
 
+
 DH = 128
 BLKTOK = 128
 RECENT = 2
@@ -38,13 +39,17 @@
     return (lax.all_gather(value, axis),)
 
 
+def near(value):
+    return pltpu.with_memory_space_constraint(value, pltpu.VMEM)
+
+
 def pieces_of(refs, count):
     if len(refs) == count:
         return [ref[...] for ref in refs]
     return [refs[0][at] for at in range(count)]
 
 
-def source_of(index, count, flips, at):
+def source_of(index, flips, at):
     return index ^ at if flips else jnp.int32(at)
 
 
@@ -75,20 +80,23 @@
     heavy_hbm,
     req_hbm,
     head_hbm,
+    dest_hbm,
     query_hbm,
     keys_hbm,
     values_hbm,
     refill_hbm,
     part_ref,
     block_ref,
+    route_ref,
+    refill,
     lengths,
     heavy,
     req,
     unit_head,
+    dest,
     query,
     keys,
     values,
-    refill,
     sems,
 ):
     pairs = (
@@ -96,6 +104,7 @@
         (heavy_hbm, heavy),
         (req_hbm, req),
         (head_hbm, unit_head),
+        (dest_hbm, dest),
         (query_hbm, query),
         (keys_hbm, keys),
         (refill_hbm, refill),
@@ -123,8 +132,25 @@
     lane = lax.broadcasted_iota(jnp.int32, (1, seq_local), 1)
     position = lane + seq_index * seq_local
     lane_block = lax.div(lane, BLKTOK)
-    for copy in copies[:4]:
+    for copy in copies[:5]:
         copy.wait()
+    seq_count = lax.axis_size("seq")
+    origin = jnp.zeros((1, LANES), jnp.int32)
+    route_lane = lax.broadcasted_iota(jnp.int32, (1, LANES), 1)
+    for u in range(held):
+        steps = lax.rem(dest[u] - seq_index + seq_count, seq_count)
+        origin = jnp.where(
+            route_lane == u, lax.rem(seq_index - steps + seq_count, seq_count), origin
+        )
+    steps = lax.rem(dest[0] - seq_index + seq_count, seq_count)
+    source = lax.rem(seq_index - steps + seq_count, seq_count)
+    wanted = lax.rem((seq_index ^ 1) - steps + seq_count, seq_count)
+    route_row = lax.broadcasted_iota(jnp.int32, (8, LANES), 0)
+    route = jnp.broadcast_to(origin, (8, LANES))
+    route = jnp.where(route_row == 1, (wanted == seq_index).astype(jnp.int32), route)
+    route = jnp.where(route_row == 2, (source == seq_index).astype(jnp.int32), route)
+    far = seq_index ^ (seq_count // 2)
+    route_ref[...] = jnp.where(route_row == 3, (source == far).astype(jnp.int32), route)
     kept = None
     for b in range(requests):
         length = lengths[b]
@@ -141,12 +167,12 @@
         kept = kept_b if kept is None else jnp.where(row_req == b, kept_b, kept)
     kept = kept > 0
 
-    copies[4].wait()
+    copies[5].wait()
     q_wide = query[...].astype(jnp.float32)
     q_rows = jnp.concatenate(
         [q_wide[:, i * DH : (i + 1) * DH] for i in range(heads_local)], axis=0
     ).astype(jnp.bfloat16)
-    copies[5].wait()
+    copies[6].wait()
     scores = []
     for g in range(kv_local):
         q_group = q_rows[g * group_rows : (g + 1) * group_rows]
@@ -160,7 +186,7 @@
     masked = jnp.where(kept, scores, NEG_BIG)
     best = jnp.max(masked, axis=1, keepdims=True)
 
-    copies[6].wait()
+    copies[7].wait()
     unit_masked, unit_on = [], []
     for u in range(held):
         on = (row_group == unit_head[u]) & (row_req == req[u])
@@ -188,7 +214,7 @@
         unit_probs.append(weight.astype(jnp.bfloat16))
     stats = jnp.where(stat_lane == 1, total, stats)
 
-    copies[7].wait()
+    copies[8].wait()
     accum = []
     for g in range(kv_local):
         probs_group = probs[g * group_rows : (g + 1) * group_rows]
@@ -212,10 +238,9 @@
     part_ref[rows:, :rows] = turned[:stat_rows]
 
 
-def middle_kernel(flips, count, rows, requests, blocks_local, dest, *refs):
-    part_refs = refs[:-3]
-    block_ref, head_ref, recall_ref = refs[-3:]
-    held = dest.shape[0]
+def middle_kernel(flips, count, rows, requests, blocks_local, held, *refs):
+    route_ref, block_ref, head_ref, recall_ref = refs[-4:]
+    part_refs = refs[:-4]
     seq_index = lax.axis_index("seq")
     pieces = pieces_of(part_refs, count)
     stat_rows = pieces[0].shape[0] - rows
@@ -227,16 +252,12 @@
     accum = tree_sum(piece[:rows] * factor for piece, factor in zip(pieces, factors))
     head_ref[:rows, :] = (accum / total).astype(jnp.bfloat16)
 
-    lane = lax.broadcasted_iota(jnp.int32, (1, held), 1)
-    origin = jnp.zeros((1, held), jnp.int32)
-    for j in range(held):
-        steps = lax.rem(dest[j, 0] - seq_index + count, count)
-        origin = jnp.where(lane == j, lax.rem(seq_index - steps + count, count), origin)
+    origin = route_ref[0:1, :held]
     recall = jnp.zeros((1, held), jnp.float32)
     for at in range(count):
         share = stats[at][:, 2 : 2 + held] * factors[at] / total
         mass = jnp.sum(share, axis=0, keepdims=True)
-        recall = jnp.where(origin == source_of(seq_index, count, flips, at), mass, recall)
+        recall = jnp.where(origin == source_of(seq_index, flips, at), mass, recall)
     recall_ref[...] = recall
 
     if flips:
@@ -261,14 +282,35 @@
     head_ref[rows:, :] = packed.astype(jnp.bfloat16)
 
 
-def final_kernel(flips, count, rows, requests, acc_ref, *refs):
-    piece_refs = refs[:-2]
-    out_ref, block_ref = refs[-2:]
+def hop_kernel(route_ref, own_ref, across_ref, out_ref):
+    keep = route_ref[1:2] > 0
+    for u in range(out_ref.shape[0]):
+        for half in range(out_ref.shape[1]):
+            out_ref[u, half] = jnp.where(keep, own_ref[u, half], across_ref[u, half])
+
+
+def place_blocks(route_ref, own_ref, across_ref, beside_ref, out_ref):
+    own, across = route_ref[2:3] > 0, route_ref[3:4] > 0
+    for u in range(out_ref.shape[0]):
+        for half in range(out_ref.shape[1]):
+            moved = jnp.where(across, across_ref[u, half], beside_ref[u, half])
+            out_ref[u, half] = jnp.where(own, own_ref[u, half], moved)
+
+
+def final_kernel(flips, count, rows, requests, routed, acc_ref, recall_in, *refs):
+    piece_refs = refs[: count if flips else 1]
+    refs = refs[len(piece_refs) :]
+    if routed:
+        out_ref, block_ref, recall_ref, kv_ref = refs[4:]
+        place_blocks(*refs[:4], kv_ref)
+    else:
+        out_ref, block_ref, recall_ref = refs
+    recall_ref[...] = recall_in[...]
     head_index = lax.axis_index("head")
     blocks_local = acc_ref.shape[1]
     pieces = pieces_of(piece_refs, count)
     for at, piece in enumerate(pieces):
-        start = source_of(head_index, count, flips, at) * rows
+        start = source_of(head_index, flips, at) * rows
         out_ref[pl.ds(pl.multiple_of(start, rows), rows), :] = piece[:rows]
     masses = []
     for piece in pieces:
@@ -289,19 +331,6 @@
 def move_blocks(refill_kv, owners, seq_index, seq_count):
     held = refill_kv.shape[0]
     steps = (owners - seq_index) % seq_count
-    if held == CAP and seq_count == 1 << CAP:
-        step = steps[0]
-        high, low = seq_count // 2, 1
-        across = flip(refill_kv, "seq", high)
-        wanted = ((seq_index ^ low) - step) % seq_count
-        passed = jnp.where(wanted == seq_index, refill_kv, across)
-        beside = flip(passed, "seq", low)
-        source = (seq_index - step) % seq_count
-        return jnp.where(
-            source == seq_index,
-            refill_kv,
-            jnp.where(source == seq_index ^ high, across, beside),
-        )
     earlier = jnp.arange(held)[:, None] > jnp.arange(held)[None, :]
     order_in = jnp.sum((owners[:, None] == owners[None, :]) & earlier, axis=1)
     slots = seq_count * CAP
@@ -340,51 +369,78 @@
     seq_index = lax.axis_index("seq")
     hbm = pl.BlockSpec(memory_space=pl.ANY)
     vmem = pl.BlockSpec(memory_space=pltpu.VMEM)
-    smem = pl.BlockSpec(memory_space=pltpu.SMEM)
     stat_rows = round_up(2 + held, 8)
-    inputs = (lengths, heavy, refill_req, refill_head, query, cache_keys, cache_values, refill_kv)
-
-    recalled_kv = move_blocks(refill_kv, refill_dest[:, 0], seq_index, seq_count)
-
-    part, block_part = pl.pallas_call(
+    scalars = (lengths, heavy, refill_req, refill_head, refill_dest.reshape(held))
+    arrays = (query, cache_keys, cache_values)
+    routed = held == CAP and seq_count == 1 << CAP
+
+    if routed:
+        across = flip(refill_kv, "seq", seq_count // 2)
+    else:
+        recalled_kv = move_blocks(refill_kv, refill_dest[:, 0], seq_index, seq_count)
+
+    part, block_part, route, own = pl.pallas_call(
         local_kernel,
         out_shape=(
-            jax.ShapeDtypeStruct((rows + stat_rows, LANES), jnp.float32),
-            jax.ShapeDtypeStruct((rows, LANES), jnp.float32),
+            pltpu.VMEM((rows + stat_rows, LANES), jnp.float32),
+            pltpu.VMEM((rows, LANES), jnp.float32),
+            pltpu.VMEM((8, LANES), jnp.int32),
+            pltpu.VMEM(refill_kv.shape, refill_kv.dtype),
         ),
-        in_specs=[hbm] * len(inputs),
-        out_specs=(vmem, vmem),
-        scratch_shapes=[pltpu.SMEM(value.shape, value.dtype) for value in inputs[:4]]
-        + [pltpu.VMEM(value.shape, value.dtype) for value in inputs[4:]]
-        + [pltpu.SemaphoreType.DMA((len(inputs),))],
+        in_specs=[hbm] * (len(scalars) + len(arrays) + 1),
+        out_specs=(vmem,) * 4,
+        scratch_shapes=[pltpu.SMEM(value.shape, value.dtype) for value in scalars]
+        + [pltpu.VMEM(value.shape, value.dtype) for value in arrays]
+        + [pltpu.SemaphoreType.DMA((len(scalars) + len(arrays) + 1,))],
         name="local_attention",
-    )(*inputs)
+    )(*scalars, *arrays, refill_kv)
 
     parts = exchange(part, "seq")
+    if routed:
+        passed = pl.pallas_call(
+            hop_kernel,
+            out_shape=pltpu.VMEM(refill_kv.shape, refill_kv.dtype),
+            in_specs=[vmem] * 3,
+            out_specs=vmem,
+            name="pick_hop",
+        )(near(route), near(own), near(across))
+        beside = flip(passed, "seq", 1)
     head_part, recall_scores = pl.pallas_call(
         functools.partial(
-            middle_kernel, by_flips(seq_count), seq_count, rows, requests, blocks_local
+            middle_kernel, by_flips(seq_count), seq_count, rows, requests, blocks_local, held
         ),
         out_shape=(
-            jax.ShapeDtypeStruct((rows + 16, LANES), jnp.bfloat16),
-            jax.ShapeDtypeStruct((1, held), jnp.float32),
+            pltpu.VMEM((rows + 16, LANES), jnp.bfloat16),
+            pltpu.VMEM((1, held), jnp.float32),
         ),
-        in_specs=[smem] + [vmem] * (len(parts) + 1),
+        in_specs=[vmem] * (len(parts) + 2),
         out_specs=(vmem, vmem),
         name="combine_seq",
-    )(refill_dest, *parts, block_part)
+    )(*(near(value) if by_flips(seq_count) else value for value in parts), near(route), near(block_part))
 
     head_parts = exchange(head_part, "head")
-    attn_rows, block_scores = pl.pallas_call(
-        functools.partial(final_kernel, by_flips(head_count), head_count, rows, requests),
-        out_shape=(
-            jax.ShapeDtypeStruct((head_count * rows, LANES), jnp.bfloat16),
-            jax.ShapeDtypeStruct(acc_scores.shape, jnp.float32),
-        ),
-        in_specs=[vmem] * (len(head_parts) + 1),
-        out_specs=(vmem, vmem),
+    blocks = (route, own, across, beside) if routed else ()
+    outputs = (
+        jax.ShapeDtypeStruct((head_count * rows, LANES), jnp.bfloat16),
+        jax.ShapeDtypeStruct(acc_scores.shape, jnp.float32),
+        jax.ShapeDtypeStruct((1, held), jnp.float32),
+        jax.ShapeDtypeStruct(refill_kv.shape, refill_kv.dtype),
+    )[: 4 if routed else 3]
+    joined = pl.pallas_call(
+        functools.partial(final_kernel, by_flips(head_count), head_count, rows, requests, routed),
+        out_shape=outputs,
+        in_specs=[vmem] * (len(head_parts) + len(blocks) + 2),
+        out_specs=(vmem,) * len(outputs),
         name="join_heads",
-    )(acc_scores, *head_parts)
+    )(
+        acc_scores,
+        near(recall_scores),
+        *(near(value) for value in head_parts),
+        *(near(value) for value in blocks),
+    )
+    attn_rows, block_scores, recall_scores = joined[:3]
+    if routed:
+        recalled_kv = joined[3]
     attn_out = (
         attn_rows.reshape(head_count * heads_local, requests, DH)
         .transpose(1, 0, 2)
@@ -412,6 +468,7 @@
         P(("groups", "seq", "head"), None, None, None),
         P(("groups", "seq", "head"), None),
     )
+
     return jax.shard_map(
         on_device, mesh=mesh, in_specs=in_specs, out_specs=out_specs, check_vma=False
     )

time: 34.6 us -> 25.7 us (0.74); the launches traced: 33.9 us -> 25.5 us
  waiting for transfers between devices: 12.4 us -> 9.7 us
  local copies, waits for them, and re-layouts: 2.53 us -> 0 us
  Pallas kernels: 5.81 us -> 3.84 us
  other arithmetic: 1.61 us -> 0 us
  starting transfers between devices: 10.8 us -> 11.3 us
    ppermute x8, waiting for transfers between devices: 12.4 us -> 9.7 us  [flip(): return lax.ppermute(value, axis, [(at, at ^ mask) for at in range(count)])]
    unnamed x17 -> x0, local copies, waits for them, and re-layouts: 2.53 us -> none
    select_n x3 -> x0, other arithmetic: 1.61 us -> none  [the longest x1 0.92 us: move_blocks(): passed = jnp.where(wanted == seq_index, refill_kv, across)]
    pallas_call x1, Pallas kernels: 1.95 us -> 0.59 us  [on_device(): pl.pallas_call(functools.partial(middle_kernel, by_flips(seq_count), seq_...]
    pallas_call x1 -> x2, Pallas kernels: 2.42 us -> 1.86 us  [the longest x1 1.82 us: on_device(): pl.pallas_call(local_kernel, out_shape=(pltpu.VMEM((rows + stat_rows, LAN...]
    ppermute x8, starting transfers between devices: 10.8 us -> 11.3 us  [flip(): return lax.ppermute(value, axis, [(at, at ^ mask) for at in range(count)])]
  transfers between devices with their start and end apart: 8 -> 8, of which waited for: 5 -> 5; matrix products, arithmetic and copies ran while one was open for 2% -> 0% of each run, Pallas kernels for 17% -> 9%
where the time goes in v2:
time: 25.7 us; the launch traced here: 25.5 us
  starting transfers between devices  11.3 us (44%)
  waiting for transfers between devices  9.7 us (38%)
  Pallas kernels  3.84 us (15%)
  between operations  0.66 us (3%)
    ppermute x8, starting transfers between devices, flip(): return lax.ppermute(value, axis, [(at, at ^ mask) for at in range(count)])  11.3 us
    ppermute x8, waiting for transfers between devices, flip(): return lax.ppermute(value, axis, [(at, at ^ mask) for at in range(count)])  9.7 us
    pallas_call x1, Pallas kernels, on_device(): pl.pallas_call(local_kernel, out_shape=(pltpu.VMEM((rows + stat_rows, LAN...  1.82 us
    pallas_call x1, Pallas kernels, on_device(): pl.pallas_call(functools.partial(final_kernel, by_flips(head_count), head...  1.39 us
    pallas_call x1, Pallas kernels, on_device(): pl.pallas_call(functools.partial(middle_kernel, by_flips(seq_count), seq_...  0.59 us
  transfers between devices with their start and end apart: 8, of which 5 were waited for; matrix products, arithmetic and copies ran while one was open for 0% of the time, Pallas kernels for 9%

profile of v2, /device:TPU:0, one launch (start us, length us, event | category | flops | bytes accessed | tf_op | source)
XLA Modules:
  0.0 25.5 jit_solution(14206216686409087786)
XLA Ops:
  0.6 4.1 %collective-permute-start.6 = (bf16[2,2,128,128]{3,2,1,0:T(8,128)(2,1)}, bf16[2,2,128,128]{3,2,1,0:T(8,128)(2,1)S(1)}, u32[]{:S(2)}, u32[]{:S(2)}) collective-permute-start(bf16[2,2,128,128]{3,2,1,0:T(8,128)(2,1)} %refill_hbm.1), channel_id=1, source_target_pairs={{0,8},{4,12},{8,0},{12,4},{1,9},{5,13},{9,1},{13,5},{2,10},{6,14},... | collective-permute-start | bytes 393224 | tf_op jit(solution)/shard_map/ppermute | solution.py:32
  4.8 1.8 %local_attention.1 = (f32[40,128]{1,0:T(8,128)S(1)}, f32[32,128]{1,0:T(8,128)S(1)}, s32[8,128]{1,0:T(8,128)S(1)}, bf16[2,2,128,128]{3,2,1,0:T(8,128)(2,1)S(1)}) custom-call(s32[2]{0:T(128)} %lengths_hbm.1, s32[2,2]{1,0:T(2,128)} %heavy_hbm.1, s32[2]{0:T(128)} %req_hbm.1, s32[2]{0:T(128)} %head_hbm.1, s32[2]{0:T(128)} %bitcast.6, bf16[2,2048]{1,0:T(2,128)(2,1)} %query_hbm.1, ...), custom_call_target="tpu_custom_call" | custom-call | tf_op jit(solution)/shard_map/local_attention/pallas_call | solution.py:382
  6.6 4.7 %collective-permute-done.6.across_ref.refs_6_ = bf16[2,2,128,128]{3,2,1,0:T(8,128)(2,1)S(1)} collective-permute-done((bf16[2,2,128,128]{3,2,1,0:T(8,128)(2,1)}, bf16[2,2,128,128]{3,2,1,0:T(8,128)(2,1)S(1)}, u32[]{:S(2)}, u32[]{:S(2)}) %collective-permute-start.6) | collective-permute-done | bytes 131104 | tf_op jit(solution)/shard_map/ppermute | solution.py:32
  11.3 0.9 %collective-permute-start.7 = (bf16[2,2,128,128]{3,2,1,0:T(8,128)(2,1)S(1)}, bf16[2,2,128,128]{3,2,1,0:T(8,128)(2,1)S(1)}, u32[]{:S(2)}, u32[]{:S(2)}) collective-permute-start(bf16[2,2,128,128]{3,2,1,0:T(8,128)(2,1)S(1)} %pick_hop.1), channel_id=1, source_target_pairs={{0,4},{4,0},{8,12},{12,8},{1,5},{5,1},{9,13},{13,9},{2,6},{6,2},{1... | collective-permute-start | bytes 393224 | tf_op jit(solution)/shard_map/ppermute | solution.py:32
  12.2 2.8 %collective-permute-start.2 = (f32[40,128]{1,0:T(8,128)S(1)}, f32[40,128]{1,0:T(8,128)S(1)}, u32[]{:S(2)}, u32[]{:S(2)}) collective-permute-start(f32[40,128]{1,0:T(8,128)S(1)} %get-tuple-element.14.refs_0_), channel_id=1, source_target_pairs={{0,12},{4,8},{8,4},{12,0},{1,13},{5,9},{9,5},{13,1},{2,14},{6,10},... | collective-permute-start | bytes 61448 | tf_op jit(solution)/shard_map/ppermute | solution.py:32
  15.0 0.5 %collective-permute-start.1 = (f32[40,128]{1,0:T(8,128)S(1)}, f32[40,128]{1,0:T(8,128)S(1)}, u32[]{:S(2)}, u32[]{:S(2)}) collective-permute-start(f32[40,128]{1,0:T(8,128)S(1)} %get-tuple-element.14.refs_0_), channel_id=1, source_target_pairs={{0,8},{4,12},{8,0},{12,4},{1,9},{5,13},{9,1},{13,5},{2,10},{6,14},... | collective-permute-start | bytes 61448 | tf_op jit(solution)/shard_map/ppermute | solution.py:32
  15.5 1.1 %collective-permute-start = (f32[40,128]{1,0:T(8,128)S(1)}, f32[40,128]{1,0:T(8,128)S(1)}, u32[]{:S(2)}, u32[]{:S(2)}) collective-permute-start(f32[40,128]{1,0:T(8,128)S(1)} %get-tuple-element.14.refs_0_), channel_id=1, source_target_pairs={{0,4},{4,0},{8,12},{12,8},{1,5},{5,1},{9,13},{13,9},{2,6},{6,2},{1... | collective-permute-start | bytes 61448 | tf_op jit(solution)/shard_map/ppermute | solution.py:32
  16.6 2.7 %collective-permute-done.2.refs_3_ = f32[40,128]{1,0:T(8,128)S(1)} collective-permute-done((f32[40,128]{1,0:T(8,128)S(1)}, f32[40,128]{1,0:T(8,128)S(1)}, u32[]{:S(2)}, u32[]{:S(2)}) %collective-permute-start.2) | collective-permute-done | bytes 20512 | tf_op jit(solution)/shard_map/ppermute | solution.py:32
  19.3 0.4 %collective-permute-done.1.refs_2_ = f32[40,128]{1,0:T(8,128)S(1)} collective-permute-done((f32[40,128]{1,0:T(8,128)S(1)}, f32[40,128]{1,0:T(8,128)S(1)}, u32[]{:S(2)}, u32[]{:S(2)}) %collective-permute-start.1) | collective-permute-done | bytes 20512 | tf_op jit(solution)/shard_map/ppermute | solution.py:32
  19.7 0.0 collective-permute-done.refs_1_
  19.7 0.6 %combine_seq.1 = (bf16[48,128]{1,0:T(8,128)(2,1)S(1)}, f32[1,2]{1,0:T(1,128)S(1)}) custom-call(f32[40,128]{1,0:T(8,128)S(1)} %get-tuple-element.14.refs_0_, f32[40,128]{1,0:T(8,128)S(1)} %collective-permute-done.refs_1_, f32[40,128]{1,0:T(8,128)S(1)} %collective-permute-done.1.refs_2_, f32[40,128]{1,0:T(8,128)S(1)} %collective-permute-done.2.refs_3_, ...), custom_call_target="tpu_custom_call" | custom-call | tf_op jit(solution)/shard_map/combine_seq/pallas_call | solution.py:408
  20.3 0.0 collective-permute-start.5
  20.3 1.6 %collective-permute-start.4 = (bf16[48,128]{1,0:T(8,128)(2,1)S(1)}, bf16[48,128]{1,0:T(8,128)(2,1)S(1)}, u32[]{:S(2)}, u32[]{:S(2)}) collective-permute-start(bf16[48,128]{1,0:T(8,128)(2,1)S(1)} %get-tuple-element.18.refs_0_), channel_id=1, source_target_pairs={{0,2},{1,3},{2,0},{3,1},{4,6},{5,7},{6,4},{7,5},{8,10},{9,11},{10,... | collective-permute-start | bytes 36872 | tf_op jit(solution)/shard_map/ppermute | solution.py:32
  21.9 0.3 %collective-permute-start.3 = (bf16[48,128]{1,0:T(8,128)(2,1)S(1)}, bf16[48,128]{1,0:T(8,128)(2,1)S(1)}, u32[]{:S(2)}, u32[]{:S(2)}) collective-permute-start(bf16[48,128]{1,0:T(8,128)(2,1)S(1)} %get-tuple-element.18.refs_0_), channel_id=1, source_target_pairs={{0,1},{1,0},{2,3},{3,2},{4,5},{5,4},{6,7},{7,6},{8,9},{9,8},{10,11... | collective-permute-start | bytes 36872 | tf_op jit(solution)/shard_map/ppermute | solution.py:32
  22.2 1.3 %collective-permute-done.5.refs_3_ = bf16[48,128]{1,0:T(8,128)(2,1)S(1)} collective-permute-done((bf16[48,128]{1,0:T(8,128)(2,1)S(1)}, bf16[48,128]{1,0:T(8,128)(2,1)S(1)}, u32[]{:S(2)}, u32[]{:S(2)}) %collective-permute-start.5) | collective-permute-done | bytes 12320 | tf_op jit(solution)/shard_map/ppermute | solution.py:32
  23.5 0.6 %collective-permute-done.4.refs_2_ = bf16[48,128]{1,0:T(8,128)(2,1)S(1)} collective-permute-done((bf16[48,128]{1,0:T(8,128)(2,1)S(1)}, bf16[48,128]{1,0:T(8,128)(2,1)S(1)}, u32[]{:S(2)}, u32[]{:S(2)}) %collective-permute-start.4) | collective-permute-done | bytes 12320 | tf_op jit(solution)/shard_map/ppermute | solution.py:32
  24.1 0.0 collective-permute-done.3.refs_1_
  24.1 0.0 collective-permute-done.7.refs_7_
  24.1 1.4 %join_heads.1 = (bf16[128,128]{1,0:T(8,128)(2,1)}, f32[2,2]{1,0:T(2,128)}, f32[1,2]{1,0:T(1,128)}, bf16[2,2,128,128]{3,2,1,0:T(8,128)(2,1)}) custom-call(f32[2,2]{1,0:T(2,128)} %acc_ref.1, f32[1,2]{1,0:T(1,128)S(1)} %get-tuple-element.17.recall_in, bf16[48,128]{1,0:T(8,128)(2,1)S(1)} %get-tuple-element.18.refs_0_, ...), custom_call_target="tpu_custom_call" | custom-call | tf_op jit(solution)/shard_map/join_heads/pallas_call | solution.py:429
  (1 shorter events, 0.0 us)
Async XLA Ops:
  0.6 10.6 %collective-permute-start.6 = (bf16[2,2,128,128]{3,2,1,0:T(8,128)(2,1)}, bf16[2,2,128,128]{3,2,1,0:T(8,128)(2,1)S(1)}, u32[]{:S(2)}, u32[]{:S(2)}) collective-permute-start(bf16[2,2,128,128]{3,2,1,0:T(8,128)(2,1)} %refill_hbm.1), channel_id=1, source_target_pairs={{0,8},{4,12},{8,0},{12,4},{1,9},{5,13},{9,1},{13,5},{2,10},{6,14},... | collective-permute-start | bytes 393224 | tf_op jit(solution)/shard_map/ppermute | solution.py:32
  11.3 12.8 %collective-permute-start.7 = (bf16[2,2,128,128]{3,2,1,0:T(8,128)(2,1)S(1)}, bf16[2,2,128,128]{3,2,1,0:T(8,128)(2,1)S(1)}, u32[]{:S(2)}, u32[]{:S(2)}) collective-permute-start(bf16[2,2,128,128]{3,2,1,0:T(8,128)(2,1)S(1)} %pick_hop.1), channel_id=1, source_target_pairs={{0,4},{4,0},{8,12},{12,8},{1,5},{5,1},{9,13},{13,9},{2,6},{6,2},{1... | collective-permute-start | bytes 393224 | tf_op jit(solution)/shard_map/ppermute | solution.py:32
  12.2 7.1 %collective-permute-start.2 = (f32[40,128]{1,0:T(8,128)S(1)}, f32[40,128]{1,0:T(8,128)S(1)}, u32[]{:S(2)}, u32[]{:S(2)}) collective-permute-start(f32[40,128]{1,0:T(8,128)S(1)} %get-tuple-element.14.refs_0_), channel_id=1, source_target_pairs={{0,12},{4,8},{8,4},{12,0},{1,13},{5,9},{9,5},{13,1},{2,14},{6,10},... | collective-permute-start | bytes 61448 | tf_op jit(solution)/shard_map/ppermute | solution.py:32
  15.0 4.7 %collective-permute-start.1 = (f32[40,128]{1,0:T(8,128)S(1)}, f32[40,128]{1,0:T(8,128)S(1)}, u32[]{:S(2)}, u32[]{:S(2)}) collective-permute-start(f32[40,128]{1,0:T(8,128)S(1)} %get-tuple-element.14.refs_0_), channel_id=1, source_target_pairs={{0,8},{4,12},{8,0},{12,4},{1,9},{5,13},{9,1},{13,5},{2,10},{6,14},... | collective-permute-start | bytes 61448 | tf_op jit(solution)/shard_map/ppermute | solution.py:32
  15.5 4.2 %collective-permute-start = (f32[40,128]{1,0:T(8,128)S(1)}, f32[40,128]{1,0:T(8,128)S(1)}, u32[]{:S(2)}, u32[]{:S(2)}) collective-permute-start(f32[40,128]{1,0:T(8,128)S(1)} %get-tuple-element.14.refs_0_), channel_id=1, source_target_pairs={{0,4},{4,0},{8,12},{12,8},{1,5},{5,1},{9,13},{13,9},{2,6},{6,2},{1... | collective-permute-start | bytes 61448 | tf_op jit(solution)/shard_map/ppermute | solution.py:32
  20.3 3.2 %collective-permute-start.5 = (bf16[48,128]{1,0:T(8,128)(2,1)S(1)}, bf16[48,128]{1,0:T(8,128)(2,1)S(1)}, u32[]{:S(2)}, u32[]{:S(2)}) collective-permute-start(bf16[48,128]{1,0:T(8,128)(2,1)S(1)} %get-tuple-element.18.refs_0_), channel_id=1, source_target_pairs={{0,3},{1,2},{2,1},{3,0},{4,7},{5,6},{6,5},{7,4},{8,11},{9,10},{10,... | collective-permute-start | bytes 36872 | tf_op jit(solution)/shard_map/ppermute | solution.py:32
  20.3 3.8 %collective-permute-start.4 = (bf16[48,128]{1,0:T(8,128)(2,1)S(1)}, bf16[48,128]{1,0:T(8,128)(2,1)S(1)}, u32[]{:S(2)}, u32[]{:S(2)}) collective-permute-start(bf16[48,128]{1,0:T(8,128)(2,1)S(1)} %get-tuple-element.18.refs_0_), channel_id=1, source_target_pairs={{0,2},{1,3},{2,0},{3,1},{4,6},{5,7},{6,4},{7,5},{8,10},{9,11},{10,... | collective-permute-start | bytes 36872 | tf_op jit(solution)/shard_map/ppermute | solution.py:32
  21.9 2.2 %collective-permute-start.3 = (bf16[48,128]{1,0:T(8,128)(2,1)S(1)}, bf16[48,128]{1,0:T(8,128)(2,1)S(1)}, u32[]{:S(2)}, u32[]{:S(2)}) collective-permute-start(bf16[48,128]{1,0:T(8,128)(2,1)S(1)} %get-tuple-element.18.refs_0_), channel_id=1, source_target_pairs={{0,1},{1,0},{2,3},{3,2},{4,5},{5,4},{6,7},{7,6},{8,9},{9,8},{10,11... | collective-permute-start | bytes 36872 | tf_op jit(solution)/shard_map/ppermute | solution.py:32

commit v3 on v2

--- a/solution.py
+++ b/solution.py
@@ -14,28 +14,72 @@
 RECENT = 2
 CAP = 2
 LANES = 128
-FEW = 8
+FEW = 4
 
 NEG_BIG = -1e30
+
+
+ORDER = (5, 6, 7, 8, 9, 3, 2, 0, 4, 1)
 
 
 def round_up(value, step):
     return (value + step - 1) // step * step
 
 
-def by_flips(count):
+def modulo(value, count):
+    if count & (count - 1) == 0:
+        return value & (count - 1)
+    return lax.rem(value + count, jnp.full_like(value, count))
+
+
+def quotient(value, count):
+    if count & (count - 1) == 0:
+        return value >> (count.bit_length() - 1)
+    return lax.div(value, jnp.full_like(value, count))
+
+
+def by_shifts(count):
     return 1 < count <= FEW and count & (count - 1) == 0
 
 
 def flip(value, axis, mask):
     count = lax.axis_size(axis)
-    return lax.ppermute(value, axis, [(at, at ^ mask) for at in range(count)])
+    return send(value, axis, [at ^ mask for at in range(count)])
+
+
+def send(value, axis, targets):
+    return lax.ppermute(value, axis, list(enumerate(targets)))
+
+
+def plan_of(axis, count):
+    if axis == "seq":
+        shifts = [count // 2] + [at for at in range(1, count) if at != count // 2]
+    else:
+        shifts = [count - 1] + list(range(1, count - 1))
+    return [[(at + shift) % count for at in range(count)] for shift in shifts]
+
+
+def sources_of(axis, count):
+    if not by_shifts(count):
+        return [[at] * count for at in range(count)]
+    return [list(range(count))] + [
+        [targets.index(at) for at in range(count)] for targets in plan_of(axis, count)
+    ]
+
+
+def in_pairs(sources):
+    order = [0]
+    for at in range(1, len(sources)):
+        if all(sources[at][sources[at][me]] == me for me in range(len(sources[at]))):
+            order.append(at)
+    return order[:2] + [at for at in range(1, len(sources)) if at not in order[:2]]
 
 
 def exchange(value, axis):
     count = lax.axis_size(axis)
-    if by_flips(count):
-        return (value,) + tuple(flip(value, axis, mask) for mask in range(1, count))
+    if by_shifts(count):
+        plan = plan_of(axis, count)
+        return (value,) + tuple(send(value, axis, targets) for targets in plan)
     return (lax.all_gather(value, axis),)
 
 
@@ -49,8 +93,15 @@
     return [refs[0][at] for at in range(count)]
 
 
-def source_of(index, flips, at):
-    return index ^ at if flips else jnp.int32(at)
+def source_of(index, sources):
+    count = len(sources)
+    for mask in range(count):
+        if all(source == at ^ mask for at, source in enumerate(sources)):
+            return index ^ mask
+    found = jnp.int32(sources[0])
+    for at in range(1, count):
+        found = jnp.where(index == at, sources[at], found)
+    return found
 
 
 def tree_sum(values):
@@ -75,104 +126,64 @@
     )
 
 
-def local_kernel(
-    lengths_hbm,
-    heavy_hbm,
-    req_hbm,
-    head_hbm,
-    dest_hbm,
-    query_hbm,
-    keys_hbm,
-    values_hbm,
-    refill_hbm,
-    part_ref,
-    block_ref,
-    route_ref,
-    refill,
-    lengths,
-    heavy,
-    req,
-    unit_head,
-    dest,
-    query,
-    keys,
-    values,
-    sems,
-):
-    pairs = (
-        (lengths_hbm, lengths),
-        (heavy_hbm, heavy),
-        (req_hbm, req),
-        (head_hbm, unit_head),
-        (dest_hbm, dest),
-        (query_hbm, query),
-        (keys_hbm, keys),
-        (refill_hbm, refill),
-        (values_hbm, values),
-    )
-    copies = [pltpu.make_async_copy(src, dst, sems.at[at]) for at, (src, dst) in enumerate(pairs)]
-    for copy in copies:
-        copy.start()
+def local_kernel(*refs):
+    count = (len(refs) - 4) // 2
+    sources, sems = refs[:count], refs[-1]
+    part_ref, block_ref, route_ref = refs[count : count + 3]
+    held_refs = refs[count + 3 : -1]
+    copies = []
+    for at in ORDER:
+        copies.append(pltpu.make_async_copy(sources[at], held_refs[at], sems.at[at]))
+        copies[-1].start()
+    copies = dict(zip(ORDER, copies))
+    refill, _, query, keys, values, lengths, heavy, req, unit_head, dest = held_refs
+    for at in (5, 6, 7, 8, 9):
+        copies[at].wait()
     requests, width = query.shape
     heads_local = width // DH
     seq_local = keys.shape[1]
     kv_local = keys.shape[2] // DH
     per_group = heads_local // kv_local
     held = refill.shape[0]
-    nheavy = heavy.shape[1]
     blocks_local = seq_local // BLKTOK
     rows = heads_local * requests
     group_rows = per_group * requests
     score_scale = 1.0 / math.sqrt(DH)
     seq_index = lax.axis_index("seq")
+    seq_count = lax.axis_size("seq")
+
+    origin = modulo(seq_index - modulo(dest[...] - seq_index, seq_count), seq_count)
+    source = origin[:, 0:1]
+    wanted = modulo(source - seq_index + (seq_index ^ 1), seq_count)
+    far = seq_index ^ (seq_count // 2)
+    route_ref[0:1, :held] = origin
+    for line, flag in enumerate((wanted == seq_index, source == seq_index, source == far)):
+        value = jnp.broadcast_to(flag.astype(jnp.int32), (1, LANES))
+        route_ref[line + 1 : line + 2, :] = value
 
     row = lax.broadcasted_iota(jnp.int32, (rows, 1), 0)
-    row_req = lax.rem(row, requests)
-    row_group = lax.div(row, group_rows)
+    row_req = modulo(row, requests)
+    row_group = quotient(row, group_rows)
     lane = lax.broadcasted_iota(jnp.int32, (1, seq_local), 1)
     position = lane + seq_index * seq_local
-    lane_block = lax.div(lane, BLKTOK)
-    for copy in copies[:5]:
-        copy.wait()
-    seq_count = lax.axis_size("seq")
-    origin = jnp.zeros((1, LANES), jnp.int32)
-    route_lane = lax.broadcasted_iota(jnp.int32, (1, LANES), 1)
-    for u in range(held):
-        steps = lax.rem(dest[u] - seq_index + seq_count, seq_count)
-        origin = jnp.where(
-            route_lane == u, lax.rem(seq_index - steps + seq_count, seq_count), origin
-        )
-    steps = lax.rem(dest[0] - seq_index + seq_count, seq_count)
-    source = lax.rem(seq_index - steps + seq_count, seq_count)
-    wanted = lax.rem((seq_index ^ 1) - steps + seq_count, seq_count)
-    route_row = lax.broadcasted_iota(jnp.int32, (8, LANES), 0)
-    route = jnp.broadcast_to(origin, (8, LANES))
-    route = jnp.where(route_row == 1, (wanted == seq_index).astype(jnp.int32), route)
-    route = jnp.where(route_row == 2, (source == seq_index).astype(jnp.int32), route)
-    far = seq_index ^ (seq_count // 2)
-    route_ref[...] = jnp.where(route_row == 3, (source == far).astype(jnp.int32), route)
+    lane_block = quotient(position, BLKTOK)
     kept = None
     for b in range(requests):
-        length = lengths[b]
-        first_recent = lax.div(length - 1, BLKTOK) - (RECENT - 1)
-        open_block = jnp.zeros((1, seq_local), jnp.int32)
-        for j in range(blocks_local):
-            block_id = seq_index * blocks_local + j
-            hit = block_id >= first_recent
-            for t in range(nheavy):
-                hit = hit | (heavy[b, t] == block_id)
-            open_block = jnp.where(lane_block == j, hit.astype(jnp.int32), open_block)
-        kept_b = jnp.where(position < length, open_block, 0)
+        length = lengths[:, b : b + 1]
+        hit = lane_block >= quotient(length - 1, BLKTOK) - (RECENT - 1)
+        for t in range(heavy.shape[1]):
+            hit = hit | (lane_block == heavy[b : b + 1, t : t + 1])
+        kept_b = jnp.where((position < length) & hit, 1, 0)
         kept_b = jnp.broadcast_to(kept_b, (rows, seq_local))
         kept = kept_b if kept is None else jnp.where(row_req == b, kept_b, kept)
     kept = kept > 0
 
-    copies[5].wait()
+    copies[2].wait()
     q_wide = query[...].astype(jnp.float32)
     q_rows = jnp.concatenate(
         [q_wide[:, i * DH : (i + 1) * DH] for i in range(heads_local)], axis=0
     ).astype(jnp.bfloat16)
-    copies[6].wait()
+    copies[3].wait()
     scores = []
     for g in range(kv_local):
         q_group = q_rows[g * group_rows : (g + 1) * group_rows]
@@ -186,10 +197,10 @@
     masked = jnp.where(kept, scores, NEG_BIG)
     best = jnp.max(masked, axis=1, keepdims=True)
 
-    copies[7].wait()
+    copies[0].wait()
     unit_masked, unit_on = [], []
     for u in range(held):
-        on = (row_group == unit_head[u]) & (row_req == req[u])
+        on = (row_group == unit_head[:, u : u + 1]) & (row_req == req[:, u : u + 1])
         dots = nt_dot(q_rows, refill[u, 0]) * score_scale
         dots = jnp.where(on, dots, NEG_BIG)
         unit_masked.append(dots)
@@ -202,7 +213,7 @@
     block_cols = jnp.zeros((rows, LANES), jnp.float32)
     for j in range(blocks_local):
         mass = jnp.sum(probs[:, j * BLKTOK : (j + 1) * BLKTOK], axis=1, keepdims=True)
-        block_cols = jnp.where(lax.rem(stat_lane, blocks_local) == j, mass, block_cols)
+        block_cols = jnp.where(modulo(stat_lane, blocks_local) == j, mass, block_cols)
     block_ref[...] = block_cols
     stats = jnp.where(stat_lane == 0, best, 0.0)
     unit_probs = []
@@ -214,7 +225,8 @@
         unit_probs.append(weight.astype(jnp.bfloat16))
     stats = jnp.where(stat_lane == 1, total, stats)
 
-    copies[8].wait()
+    copies[4].wait()
+    copies[1].wait()
     accum = []
     for g in range(kv_local):
         probs_group = probs[g * group_rows : (g + 1) * group_rows]
@@ -238,7 +250,7 @@
     part_ref[rows:, :rows] = turned[:stat_rows]
 
 
-def middle_kernel(flips, count, rows, requests, blocks_local, held, *refs):
+def middle_kernel(shifts, count, rows, requests, blocks_local, held, *refs):
     route_ref, block_ref, head_ref, recall_ref = refs[-4:]
     part_refs = refs[:-4]
     seq_index = lax.axis_index("seq")
@@ -248,8 +260,9 @@
     stats = [turned[:rows, at * stat_rows : (at + 1) * stat_rows] for at in range(count)]
     best = functools.reduce(jnp.maximum, [stat[:, 0:1] for stat in stats])
     factors = [jnp.exp(stat[:, 0:1] - best) for stat in stats]
-    total = tree_sum(stat[:, 1:2] * factor for stat, factor in zip(stats, factors))
-    accum = tree_sum(piece[:rows] * factor for piece, factor in zip(pieces, factors))
+    order = in_pairs(sources_of("seq", count)) if shifts else range(count)
+    total = tree_sum(stats[at][:, 1:2] * factors[at] for at in order)
+    accum = tree_sum(pieces[at][:rows] * factors[at] for at in order)
     head_ref[:rows, :] = (accum / total).astype(jnp.bfloat16)
 
     origin = route_ref[0:1, :held]
@@ -257,10 +270,10 @@
     for at in range(count):
         share = stats[at][:, 2 : 2 + held] * factors[at] / total
         mass = jnp.sum(share, axis=0, keepdims=True)
-        recall = jnp.where(origin == source_of(seq_index, flips, at), mass, recall)
+        recall = jnp.where(origin == source_of(seq_index, sources_of("seq", count)[at]), mass, recall)
     recall_ref[...] = recall
 
-    if flips:
+    if shifts:
         own = factors[0]
     else:
         own = functools.reduce(
@@ -270,7 +283,7 @@
         )
     row = lax.broadcasted_iota(jnp.int32, (rows, LANES), 0)
     lanes = lax.broadcasted_iota(jnp.int32, (rows, LANES), 1)
-    mine = lax.rem(row, requests) == lax.div(lanes, blocks_local)
+    mine = modulo(row, requests) == quotient(lanes, blocks_local)
     mass = jnp.sum(jnp.where(mine, block_ref[...] * own / total, 0.0), axis=0, keepdims=True)
     high = mass.astype(jnp.bfloat16).astype(jnp.float32)
     middle = (mass - high).astype(jnp.bfloat16).astype(jnp.float32)
@@ -289,34 +302,41 @@
             out_ref[u, half] = jnp.where(keep, own_ref[u, half], across_ref[u, half])
 
 
-def place_blocks(route_ref, own_ref, across_ref, beside_ref, out_ref):
-    own, across = route_ref[2:3] > 0, route_ref[3:4] > 0
-    for u in range(out_ref.shape[0]):
-        for half in range(out_ref.shape[1]):
-            moved = jnp.where(across, across_ref[u, half], beside_ref[u, half])
-            out_ref[u, half] = jnp.where(own, own_ref[u, half], moved)
-
-
-def final_kernel(flips, count, rows, requests, routed, acc_ref, recall_in, *refs):
-    piece_refs = refs[: count if flips else 1]
+def final_kernel(shifts, count, rows, requests, routed, acc_ref, recall_ref, *refs):
+    piece_refs = refs[: count if shifts else 1]
     refs = refs[len(piece_refs) :]
+    outs = 4 if routed else 3
     if routed:
-        out_ref, block_ref, recall_ref, kv_ref = refs[4:]
-        place_blocks(*refs[:4], kv_ref)
-    else:
-        out_ref, block_ref, recall_ref = refs
-    recall_ref[...] = recall_in[...]
+        route_ref, own_ref, across_ref, beside_ref = refs[:4]
+        refs = refs[4:]
+    hbm_refs, sems = refs[:outs], refs[-1]
+    attn, block = refs[outs : outs + 2]
+    recall_copy = pltpu.make_async_copy(recall_ref, hbm_refs[2], sems.at[2])
+    recall_copy.start()
+    copies = [recall_copy]
+    if routed:
+        blocks = refs[outs + 2]
+        own, across = route_ref[2:3] > 0, route_ref[3:4] > 0
+        for u in range(blocks.shape[0]):
+            for half in range(blocks.shape[1]):
+                moved = jnp.where(across, across_ref[u, half], beside_ref[u, half])
+                blocks[u, half] = jnp.where(own, own_ref[u, half], moved)
+        copies.append(pltpu.make_async_copy(blocks, hbm_refs[3], sems.at[3]))
+        copies[-1].start()
     head_index = lax.axis_index("head")
     blocks_local = acc_ref.shape[1]
     pieces = pieces_of(piece_refs, count)
     for at, piece in enumerate(pieces):
-        start = source_of(head_index, flips, at) * rows
-        out_ref[pl.ds(pl.multiple_of(start, rows), rows), :] = piece[:rows]
+        start = source_of(head_index, sources_of("head", count)[at]) * rows
+        attn[pl.ds(pl.multiple_of(start, rows), rows), :] = piece[:rows]
+    copies.append(pltpu.make_async_copy(attn, hbm_refs[0], sems.at[0]))
+    copies[-1].start()
     masses = []
     for piece in pieces:
         lines = piece[rows:].astype(jnp.float32)
         masses.append(lines[0:1] + lines[1:2] + lines[2:3])
-    mass = tree_sum(masses)
+    order = in_pairs(sources_of("head", count)) if shifts else range(count)
+    mass = tree_sum(masses[at] for at in order)
     lanes = lax.broadcasted_iota(jnp.int32, (1, LANES), 1)
     at_req = lax.broadcasted_iota(jnp.int32, (requests, blocks_local), 0)
     at_block = lax.broadcasted_iota(jnp.int32, (requests, blocks_local), 1)
@@ -325,7 +345,11 @@
         for j in range(blocks_local):
             one = jnp.sum(jnp.where(lanes == b * blocks_local + j, mass, 0.0), axis=1, keepdims=True)
             added = jnp.where((at_req == b) & (at_block == j), added + one, added)
-    block_ref[...] = added
+    block[...] = added
+    copies.append(pltpu.make_async_copy(block, hbm_refs[1], sems.at[1]))
+    copies[-1].start()
+    for copy in copies:
+        copy.wait()
 
 
 def move_blocks(refill_kv, owners, seq_index, seq_count):
@@ -370,8 +394,19 @@
     hbm = pl.BlockSpec(memory_space=pl.ANY)
     vmem = pl.BlockSpec(memory_space=pltpu.VMEM)
     stat_rows = round_up(2 + held, 8)
-    scalars = (lengths, heavy, refill_req, refill_head, refill_dest.reshape(held))
-    arrays = (query, cache_keys, cache_values)
+    row_of = lambda value: value.reshape(1, value.size)
+    inputs = (
+        refill_kv,
+        acc_scores,
+        query,
+        cache_keys,
+        cache_values,
+        row_of(lengths),
+        heavy,
+        row_of(refill_req),
+        row_of(refill_head),
+        row_of(refill_dest),
+    )
     routed = held == CAP and seq_count == 1 << CAP
 
     if routed:
@@ -379,21 +414,21 @@
     else:
         recalled_kv = move_blocks(refill_kv, refill_dest[:, 0], seq_index, seq_count)
 
-    part, block_part, route, own = pl.pallas_call(
+    part, block_part, route, own, acc = pl.pallas_call(
         local_kernel,
         out_shape=(
             pltpu.VMEM((rows + stat_rows, LANES), jnp.float32),
             pltpu.VMEM((rows, LANES), jnp.float32),
             pltpu.VMEM((8, LANES), jnp.int32),
             pltpu.VMEM(refill_kv.shape, refill_kv.dtype),
+            pltpu.VMEM(acc_scores.shape, acc_scores.dtype),
         ),
-        in_specs=[hbm] * (len(scalars) + len(arrays) + 1),
-        out_specs=(vmem,) * 4,
-        scratch_shapes=[pltpu.SMEM(value.shape, value.dtype) for value in scalars]
-        + [pltpu.VMEM(value.shape, value.dtype) for value in arrays]
-        + [pltpu.SemaphoreType.DMA((len(scalars) + len(arrays) + 1,))],
+        in_specs=[hbm] * len(inputs),
+        out_specs=(vmem,) * 5,
+        scratch_shapes=[pltpu.VMEM(value.shape, value.dtype) for value in inputs[2:]]
+        + [pltpu.SemaphoreType.DMA((len(inputs),))],
         name="local_attention",
-    )(*scalars, *arrays, refill_kv)
+    )(*inputs)
 
     parts = exchange(part, "seq")
     if routed:
@@ -407,7 +442,7 @@
         beside = flip(passed, "seq", 1)
     head_part, recall_scores = pl.pallas_call(
         functools.partial(
-            middle_kernel, by_flips(seq_count), seq_count, rows, requests, blocks_local, held
+            middle_kernel, by_shifts(seq_count), seq_count, rows, requests, blocks_local, held
         ),
         out_shape=(
             pltpu.VMEM((rows + 16, LANES), jnp.bfloat16),
@@ -416,7 +451,7 @@
         in_specs=[vmem] * (len(parts) + 2),
         out_specs=(vmem, vmem),
         name="combine_seq",
-    )(*(near(value) if by_flips(seq_count) else value for value in parts), near(route), near(block_part))
+    )(*(near(value) if by_shifts(seq_count) else value for value in parts), near(route), near(block_part))
 
     head_parts = exchange(head_part, "head")
     blocks = (route, own, across, beside) if routed else ()
@@ -427,13 +462,17 @@
         jax.ShapeDtypeStruct(refill_kv.shape, refill_kv.dtype),
     )[: 4 if routed else 3]
     joined = pl.pallas_call(
-        functools.partial(final_kernel, by_flips(head_count), head_count, rows, requests, routed),
+        functools.partial(final_kernel, by_shifts(head_count), head_count, rows, requests, routed),
         out_shape=outputs,
         in_specs=[vmem] * (len(head_parts) + len(blocks) + 2),
-        out_specs=(vmem,) * len(outputs),
+        out_specs=(hbm,) * len(outputs),
+        scratch_shapes=[
+            pltpu.VMEM(outputs[at].shape, outputs[at].dtype) for at in (0, 1, 3)[: len(outputs) - 1]
+        ]
+        + [pltpu.SemaphoreType.DMA((len(outputs),))],
         name="join_heads",
     )(
-        acc_scores,
+        near(acc),
         near(recall_scores),
         *(near(value) for value in head_parts),
         *(near(value) for value in blocks),

time: 25.7 us -> 26.9 us (1.047)
  starting transfers between devices: 11.3 us -> 13.6 us
  waiting for transfers between devices: 9.7 us -> 9.08 us
  Pallas kernels: 3.84 us -> 3.26 us
    ppermute x8, starting transfers between devices: 11.3 us -> 13.6 us  [send(): return lax.ppermute(value, axis, list(enumerate(targets)))]
    pallas_call x2, Pallas kernels: 1.98 us -> 1.34 us  [the longest x1 0.75 us: on_device(): pl.pallas_call(functools.partial(final_kernel, by_shifts(head_count), hea...]
    ppermute x8, waiting for transfers between devices: 9.7 us -> 9.08 us  [send(): return lax.ppermute(value, axis, list(enumerate(targets)))]
  transfers between devices with their start and end apart: 8 -> 8, of which waited for: 5 -> 4; matrix products, arithmetic and copies ran while one was open for 0% -> 0% of each run, Pallas kernels for 9% -> 9%
where the time goes in v3:
time: 26.9 us; the launch traced here: 26.6 us
  starting transfers between devices  13.6 us (51%)
  waiting for transfers between devices  9.08 us (34%)
  Pallas kernels  3.26 us (12%)
  between operations  0.66 us (2%)
    ppermute x8, starting transfers between devices, send(): return lax.ppermute(value, axis, list(enumerate(targets)))  13.6 us
    ppermute x8, waiting for transfers between devices, send(): return lax.ppermute(value, axis, list(enumerate(targets)))  9.08 us
    pallas_call x1, Pallas kernels, on_device(): pl.pallas_call(local_kernel, out_shape=(pltpu.VMEM((rows + stat_rows, LAN...  1.89 us
    pallas_call x1, Pallas kernels, on_device(): pl.pallas_call(functools.partial(final_kernel, by_shifts(head_count), hea...  0.75 us
    pallas_call x1, Pallas kernels, on_device(): pl.pallas_call(functools.partial(middle_kernel, by_shifts(seq_count), seq...  0.59 us
  transfers between devices with their start and end apart: 8, of which 4 were waited for; matrix products, arithmetic and copies ran while one was open for 0% of the time, Pallas kernels for 9%

profile of v3, /device:TPU:0, one launch (start us, length us, event | category | flops | bytes accessed | tf_op | source)
XLA Modules:
  0.0 26.6 jit_solution(16271487912600792741)
XLA Ops:
  0.6 4.1 %collective-permute-start.6 = (bf16[2,2,128,128]{3,2,1,0:T(8,128)(2,1)}, bf16[2,2,128,128]{3,2,1,0:T(8,128)(2,1)S(1)}, u32[]{:S(2)}, u32[]{:S(2)}) collective-permute-start(bf16[2,2,128,128]{3,2,1,0:T(8,128)(2,1)} %refs_0_.1), channel_id=1, source_target_pairs={{0,8},{4,12},{8,0},{12,4},{1,9},{5,13},{9,1},{13,5},{2,10},{6,14},... | collective-permute-start | bytes 393224 | tf_op jit(solution)/shard_map/ppermute | solution.py:51
  4.8 1.9 %local_attention.1 = (f32[40,128]{1,0:T(8,128)S(1)}, f32[32,128]{1,0:T(8,128)S(1)}, s32[8,128]{1,0:T(8,128)S(1)}, bf16[2,2,128,128]{3,2,1,0:T(8,128)(2,1)S(1)}, f32[2,2]{1,0:T(2,128)S(1)}) custom-call(bf16[2,2,128,128]{3,2,1,0:T(8,128)(2,1)} %refs_0_.1, f32[2,2]{1,0:T(2,128)} %refs_1_.1, bf16[2,2048]{1,0:T(2,128)(2,1)} %refs_2_.1, ...), custom_call_target="tpu_custom_call" | custom-call | tf_op jit(solution)/shard_map/local_attention/pallas_call | solution.py:417
  6.7 4.6 %collective-permute-done.6.across_ref.refs_6_ = bf16[2,2,128,128]{3,2,1,0:T(8,128)(2,1)S(1)} collective-permute-done((bf16[2,2,128,128]{3,2,1,0:T(8,128)(2,1)}, bf16[2,2,128,128]{3,2,1,0:T(8,128)(2,1)S(1)}, u32[]{:S(2)}, u32[]{:S(2)}) %collective-permute-start.6) | collective-permute-done | bytes 131104 | tf_op jit(solution)/shard_map/ppermute | solution.py:51
  11.3 0.9 %collective-permute-start.7 = (bf16[2,2,128,128]{3,2,1,0:T(8,128)(2,1)S(1)}, bf16[2,2,128,128]{3,2,1,0:T(8,128)(2,1)S(1)}, u32[]{:S(2)}, u32[]{:S(2)}) collective-permute-start(bf16[2,2,128,128]{3,2,1,0:T(8,128)(2,1)S(1)} %pick_hop.1), channel_id=1, source_target_pairs={{0,4},{4,0},{8,12},{12,8},{1,5},{5,1},{9,13},{13,9},{2,6},{6,2},{1... | collective-permute-start | bytes 393224 | tf_op jit(solution)/shard_map/ppermute | solution.py:51
  12.2 2.8 %collective-permute-start.2 = (f32[40,128]{1,0:T(8,128)S(1)}, f32[40,128]{1,0:T(8,128)S(1)}, u32[]{:S(2)}, u32[]{:S(2)}) collective-permute-start(f32[40,128]{1,0:T(8,128)S(1)} %get-tuple-element.16.refs_0_), channel_id=1, source_target_pairs={{0,12},{4,0},{8,4},{12,8},{1,13},{5,1},{9,5},{13,9},{2,14},{6,2},{... | collective-permute-start | bytes 61448 | tf_op jit(solution)/shard_map/ppermute | solution.py:51
  15.0 0.0 collective-permute-start.1
  15.0 2.5 %collective-permute-start = (f32[40,128]{1,0:T(8,128)S(1)}, f32[40,128]{1,0:T(8,128)S(1)}, u32[]{:S(2)}, u32[]{:S(2)}) collective-permute-start(f32[40,128]{1,0:T(8,128)S(1)} %get-tuple-element.16.refs_0_), channel_id=1, source_target_pairs={{0,8},{4,12},{8,0},{12,4},{1,9},{5,13},{9,1},{13,5},{2,10},{6,14},... | collective-permute-start | bytes 61448 | tf_op jit(solution)/shard_map/ppermute | solution.py:51
  17.5 0.0 collective-permute-done.2.refs_3_
  17.5 3.1 %collective-permute-done.1.refs_2_ = f32[40,128]{1,0:T(8,128)S(1)} collective-permute-done((f32[40,128]{1,0:T(8,128)S(1)}, f32[40,128]{1,0:T(8,128)S(1)}, u32[]{:S(2)}, u32[]{:S(2)}) %collective-permute-start.1) | collective-permute-done | bytes 20512 | tf_op jit(solution)/shard_map/ppermute | solution.py:51
  20.6 0.0 collective-permute-done.refs_1_
  20.6 0.6 %combine_seq.1 = (bf16[48,128]{1,0:T(8,128)(2,1)S(1)}, f32[1,2]{1,0:T(1,128)S(1)}) custom-call(f32[40,128]{1,0:T(8,128)S(1)} %get-tuple-element.16.refs_0_, f32[40,128]{1,0:T(8,128)S(1)} %collective-permute-done.refs_1_, f32[40,128]{1,0:T(8,128)S(1)} %collective-permute-done.1.refs_2_, f32[40,128]{1,0:T(8,128)S(1)} %collective-permute-done.2.refs_3_, ...), custom_call_target="tpu_custom_call" | custom-call | tf_op jit(solution)/shard_map/combine_seq/pallas_call | solution.py:443
  21.2 1.5 %collective-permute-start.5 = (bf16[48,128]{1,0:T(8,128)(2,1)S(1)}, bf16[48,128]{1,0:T(8,128)(2,1)S(1)}, u32[]{:S(2)}, u32[]{:S(2)}) collective-permute-start(bf16[48,128]{1,0:T(8,128)(2,1)S(1)} %get-tuple-element.20.refs_0_), channel_id=1, source_target_pairs={{0,2},{1,3},{2,0},{3,1},{4,6},{5,7},{6,4},{7,5},{8,10},{9,11},{10,... | collective-permute-start | bytes 36872 | tf_op jit(solution)/shard_map/ppermute | solution.py:51
  22.7 0.0 collective-permute-start.4
  22.7 1.7 %collective-permute-start.3 = (bf16[48,128]{1,0:T(8,128)(2,1)S(1)}, bf16[48,128]{1,0:T(8,128)(2,1)S(1)}, u32[]{:S(2)}, u32[]{:S(2)}) collective-permute-start(bf16[48,128]{1,0:T(8,128)(2,1)S(1)} %get-tuple-element.20.refs_0_), channel_id=1, source_target_pairs={{0,3},{1,0},{2,1},{3,2},{4,7},{5,4},{6,5},{7,6},{8,11},{9,8},{10,9... | collective-permute-start | bytes 36872 | tf_op jit(solution)/shard_map/ppermute | solution.py:51
  24.4 0.5 %collective-permute-done.5.refs_3_ = bf16[48,128]{1,0:T(8,128)(2,1)S(1)} collective-permute-done((bf16[48,128]{1,0:T(8,128)(2,1)S(1)}, bf16[48,128]{1,0:T(8,128)(2,1)S(1)}, u32[]{:S(2)}, u32[]{:S(2)}) %collective-permute-start.5) | collective-permute-done | bytes 12320 | tf_op jit(solution)/shard_map/ppermute | solution.py:51
  24.9 0.9 %collective-permute-done.4.refs_2_ = bf16[48,128]{1,0:T(8,128)(2,1)S(1)} collective-permute-done((bf16[48,128]{1,0:T(8,128)(2,1)S(1)}, bf16[48,128]{1,0:T(8,128)(2,1)S(1)}, u32[]{:S(2)}, u32[]{:S(2)}) %collective-permute-start.4) | collective-permute-done | bytes 12320 | tf_op jit(solution)/shard_map/ppermute | solution.py:51
  25.8 0.0 collective-permute-done.3.refs_1_
  25.8 0.0 collective-permute-done.7.refs_7_
  25.8 0.7 %join_heads.1 = (bf16[128,128]{1,0:T(8,128)(2,1)}, f32[2,2]{1,0:T(2,128)}, f32[1,2]{1,0:T(1,128)}, bf16[2,2,128,128]{3,2,1,0:T(8,128)(2,1)}) custom-call(f32[2,2]{1,0:T(2,128)S(1)} %get-tuple-element.15.acc_ref, f32[1,2]{1,0:T(1,128)S(1)} %get-tuple-element.19.recall_ref, bf16[48,128]{1,0:T(8,128)(2,1)S(1)} %get-tuple-element.20.refs_0_, ...), custom_call_target="tpu_custom_call" | custom-call | tf_op jit(solution)/shard_map/join_heads/pallas_call | solution.py:464
  (1 shorter events, 0.0 us)
Async XLA Ops:
  0.6 10.6 %collective-permute-start.6 = (bf16[2,2,128,128]{3,2,1,0:T(8,128)(2,1)}, bf16[2,2,128,128]{3,2,1,0:T(8,128)(2,1)S(1)}, u32[]{:S(2)}, u32[]{:S(2)}) collective-permute-start(bf16[2,2,128,128]{3,2,1,0:T(8,128)(2,1)} %refs_0_.1), channel_id=1, source_target_pairs={{0,8},{4,12},{8,0},{12,4},{1,9},{5,13},{9,1},{13,5},{2,10},{6,14},... | collective-permute-start | bytes 393224 | tf_op jit(solution)/shard_map/ppermute | solution.py:51
  11.3 14.5 %collective-permute-start.7 = (bf16[2,2,128,128]{3,2,1,0:T(8,128)(2,1)S(1)}, bf16[2,2,128,128]{3,2,1,0:T(8,128)(2,1)S(1)}, u32[]{:S(2)}, u32[]{:S(2)}) collective-permute-start(bf16[2,2,128,128]{3,2,1,0:T(8,128)(2,1)S(1)} %pick_hop.1), channel_id=1, source_target_pairs={{0,4},{4,0},{8,12},{12,8},{1,5},{5,1},{9,13},{13,9},{2,6},{6,2},{1... | collective-permute-start | bytes 393224 | tf_op jit(solution)/shard_map/ppermute | solution.py:51
  12.2 5.3 %collective-permute-start.2 = (f32[40,128]{1,0:T(8,128)S(1)}, f32[40,128]{1,0:T(8,128)S(1)}, u32[]{:S(2)}, u32[]{:S(2)}) collective-permute-start(f32[40,128]{1,0:T(8,128)S(1)} %get-tuple-element.16.refs_0_), channel_id=1, source_target_pairs={{0,12},{4,0},{8,4},{12,8},{1,13},{5,1},{9,5},{13,9},{2,14},{6,2},{... | collective-permute-start | bytes 61448 | tf_op jit(solution)/shard_map/ppermute | solution.py:51
  15.0 5.6 %collective-permute-start.1 = (f32[40,128]{1,0:T(8,128)S(1)}, f32[40,128]{1,0:T(8,128)S(1)}, u32[]{:S(2)}, u32[]{:S(2)}) collective-permute-start(f32[40,128]{1,0:T(8,128)S(1)} %get-tuple-element.16.refs_0_), channel_id=1, source_target_pairs={{0,4},{4,8},{8,12},{12,0},{1,5},{5,9},{9,13},{13,1},{2,6},{6,10},{... | collective-permute-start | bytes 61448 | tf_op jit(solution)/shard_map/ppermute | solution.py:51
  15.0 5.6 %collective-permute-start = (f32[40,128]{1,0:T(8,128)S(1)}, f32[40,128]{1,0:T(8,128)S(1)}, u32[]{:S(2)}, u32[]{:S(2)}) collective-permute-start(f32[40,128]{1,0:T(8,128)S(1)} %get-tuple-element.16.refs_0_), channel_id=1, source_target_pairs={{0,8},{4,12},{8,0},{12,4},{1,9},{5,13},{9,1},{13,5},{2,10},{6,14},... | collective-permute-start | bytes 61448 | tf_op jit(solution)/shard_map/ppermute | solution.py:51
  21.2 3.7 %collective-permute-start.5 = (bf16[48,128]{1,0:T(8,128)(2,1)S(1)}, bf16[48,128]{1,0:T(8,128)(2,1)S(1)}, u32[]{:S(2)}, u32[]{:S(2)}) collective-permute-start(bf16[48,128]{1,0:T(8,128)(2,1)S(1)} %get-tuple-element.20.refs_0_), channel_id=1, source_target_pairs={{0,2},{1,3},{2,0},{3,1},{4,6},{5,7},{6,4},{7,5},{8,10},{9,11},{10,... | collective-permute-start | bytes 36872 | tf_op jit(solution)/shard_map/ppermute | solution.py:51
  22.7 3.1 %collective-permute-start.4 = (bf16[48,128]{1,0:T(8,128)(2,1)S(1)}, bf16[48,128]{1,0:T(8,128)(2,1)S(1)}, u32[]{:S(2)}, u32[]{:S(2)}) collective-permute-start(bf16[48,128]{1,0:T(8,128)(2,1)S(1)} %get-tuple-element.20.refs_0_), channel_id=1, source_target_pairs={{0,1},{1,2},{2,3},{3,0},{4,5},{5,6},{6,7},{7,4},{8,9},{9,10},{10,1... | collective-permute-start | bytes 36872 | tf_op jit(solution)/shard_map/ppermute | solution.py:51
  22.7 3.1 %collective-permute-start.3 = (bf16[48,128]{1,0:T(8,128)(2,1)S(1)}, bf16[48,128]{1,0:T(8,128)(2,1)S(1)}, u32[]{:S(2)}, u32[]{:S(2)}) collective-permute-start(bf16[48,128]{1,0:T(8,128)(2,1)S(1)} %get-tuple-element.20.refs_0_), channel_id=1, source_target_pairs={{0,3},{1,0},{2,1},{3,2},{4,7},{5,4},{6,5},{7,6},{8,11},{9,8},{10,9... | collective-permute-start | bytes 36872 | tf_op jit(solution)/shard_map/ppermute | solution.py:51
